TPU v7x, 64 devices: a 2x2x8 block of a 4x4x8 slice. The times are simulated.
64 devices in a mesh: rep: 4 (over x, y), dp: 16 (over z, core).
Axes of the slice: x: 2, y: 2, z: 8, core: 2. Of those that a mesh axis runs over, the one named last changes fastest.
The devices are a block of a 4x4x8 slice.
Arguments:
- x: bfloat16 [64, 4096, 512], P(('rep', 'dp')), parts along dimension 0
- dy: bfloat16 [64, 4096, 512], P(('rep', 'dp')), parts along dimension 0
- w_gate: bfloat16 [2, 512, 1280], P(None, 'dp')
- w_up: bfloat16 [2, 512, 1280], P(None, 'dp')
- w_down: bfloat16 [2, 1280, 512], P(None, 'dp')
- m_w_gate: float32 [2, 512, 1280], P(None, 'dp')
- m_w_up: float32 [2, 512, 1280], P(None, 'dp')
- m_w_down: float32 [2, 1280, 512], P(None, 'dp')
- v_w_gate: float32 [2, 512, 1280], P(None, 'dp')
- v_w_up: float32 [2, 512, 1280], P(None, 'dp')
- v_w_down: float32 [2, 1280, 512], P(None, 'dp')
Outputs:
- output 1: bfloat16 [8, 512, 1280], P('rep', 'dp'), parts along dimension 0
- output 2: bfloat16 [8, 512, 1280], P('rep', 'dp'), parts along dimension 0
- output 3: bfloat16 [8, 1280, 512], P('rep', 'dp'), parts along dimension 0
- output 4: float32 [8, 512, 1280], P('rep', 'dp'), parts along dimension 0
- output 5: float32 [8, 512, 1280], P('rep', 'dp'), parts along dimension 0
- output 6: float32 [8, 1280, 512], P('rep', 'dp'), parts along dimension 0
- output 7: float32 [8, 512, 1280], P('rep', 'dp'), parts along dimension 0
- output 8: float32 [8, 512, 1280], P('rep', 'dp'), parts along dimension 0
- output 9: float32 [8, 1280, 512], P('rep', 'dp'), parts along dimension 0
There are 4 independent parts. A program takes and returns all parts, laid end to end along the dimension named above; an argument that names none is the same for every part.
All inputs are finite; a program needn't handle non-finite values.
Results may differ from a plain program's by a relative error of at most 0.0222.
Values are sent between devices in bfloat16 or wider.
A program may use at most 768 MiB of HBM per device.

v0:
```python
import jax
import jax.numpy as jnp
from jax import lax
from jax.sharding import PartitionSpec as P

NAMES = ("w_gate", "w_up", "w_down")


def matmul(a, w):
    return jnp.dot(a, w, preferred_element_type=jnp.float32).astype(jnp.bfloat16)


def normed(h):
    wide = h.astype(jnp.float32)
    scale = lax.rsqrt(jnp.mean(wide**2, -1, keepdims=True) + 1e-6)
    return (wide * scale).astype(jnp.bfloat16)


def layer(h, w):
    a = normed(h)
    gate = jnp.dot(a, w["w_gate"], preferred_element_type=jnp.float32)
    up = jnp.dot(a, w["w_up"], preferred_element_type=jnp.float32)
    return h + matmul((jax.nn.silu(gate) * up).astype(jnp.bfloat16), w["w_down"])


def adamw(w, m, v, g):
    m = 0.9 * m + 0.1 * g
    v = 0.95 * v + 0.05 * g * g
    step = m * lax.rsqrt(v + 1e-8) + 0.1 * w
    return (w - 0.02 * step).astype(jnp.bfloat16), m, v


def clipped(gradients, sum_of_squares, count):
    factor = jnp.minimum(1.0, 0.5 * lax.rsqrt(sum_of_squares / count + 1e-30))
    return [g * factor for g in gradients]


def solution(mesh):
    def fetched(weights, number):
        return {name: lax.all_gather(w[number], "dp", axis=0, tiled=True) for name, w in zip(NAMES, weights, strict=True)}

    def step(x, dy, *arrays):
        weights, m, v = (arrays[i : i + 3] for i in (0, 3, 6))
        layers = weights[0].shape[0]
        h, kept = x[0], []
        for number in range(layers):
            kept.append(h)
            h = layer(h, fetched(weights, number))
        by_h, mine = dy[0], [None] * layers
        for number in reversed(range(layers)):
            _, back = jax.vjp(lambda w, h: layer(h, w), fetched(weights, number), kept[number])
            by_w, by_h = back(by_h)
            mine[number] = [lax.psum_scatter(by_w[name], "dp", scatter_dimension=0, tiled=True) for name in NAMES]
        gradients = [jnp.stack([mine[number][i] for number in range(layers)]).astype(jnp.float32) for i in range(3)]
        squares = lax.psum(sum(jnp.sum(g * g) for g in gradients), "dp")
        gradients = clipped(gradients, squares, lax.psum(1, "dp") * sum(g.size for g in gradients))
        new = [adamw(w.astype(jnp.float32), m, v, g) for w, m, v, g in zip(weights, m, v, gradients, strict=True)]
        return tuple(one[which] for which in range(3) for one in new)

    states, cut = P(("rep", "dp"), None, None), P(None, "dp", None)
    return jax.shard_map(
        step,
        mesh=mesh,
        in_specs=(states, states) + (cut,) * 9,
        out_specs=(P("rep", "dp", None),) * 9,
        check_vma=False,
    )
```

profile of v0, /device:TPU:21, one launch (start us, length us, event | category | flops | bytes accessed | tf_op | source)
XLA Modules:
  0.0 646.2 jit_solution(2895646908991940027)
XLA Ops:
  7.3 1.6 fusion.93
  8.9 0.1 all-gather.15.cloned.1.call-start
  9.0 1.6 fusion.92
  10.6 0.1 all-gather.17.cloned.1.call-start
  10.7 1.6 fusion.91
  12.5 0.6 all-gather.21.cloned.1.call-update
  13.1 0.6 all-gather.23.cloned.1.call-update
  13.7 0.6 all-gather.19.cloned.1.call-update
  14.4 6.4 copy.20
  20.7 3.1 fusion.15
  23.8 6.4 copy.21
  30.2 20.6 %all-gather.13.cloned.1.call-done = bf16[1,512,1280]{2,1,0:T(8,128)(2,1)} async-done(((bf16[1,32,1280]{2,1,0:T(8,128)(2,1)}), bf16[1,512,1280]{2,1,0:T(8,128)(2,1)}) %all-gather.13.cloned.1.call-update) | async-done | bytes 1310736 | tf_op jit(solution)/shard_map/all_gather | solution.py:40
  50.8 11.9 %fusion.47 = f32[4096,1280]{1,0:T(8,128)} fusion(bf16[1,4096,512]{1,2,0:T(8,128)(2,1)} %copy.20, f32[4096]{0:T(1024)S(1)} %add_rsqrt_fusion, bf16[1,512,1280]{2,1,0:T(8,128)(2,1)} %all-gather.13.cloned.1.call-done), kind=kOutput, calls=%fused_computation.57 | convolution fusion | flops 5375000576 | bytes 26492928 | tf_op jit(solution)/shard_map/dot_general | solution.py:21
  62.7 24.3 %all-gather.15.cloned.1.call-done = bf16[1,512,1280]{2,1,0:T(8,128)(2,1)} async-done(((bf16[1,32,1280]{2,1,0:T(8,128)(2,1)}), bf16[1,512,1280]{2,1,0:T(8,128)(2,1)}) %all-gather.15.cloned.1.call-update) | async-done | bytes 1310736 | tf_op jit(solution)/shard_map/all_gather | solution.py:40
  87.0 19.1 %multiply_convert_fusion.1 = (bf16[4096,1280]{1,0:T(8,128)(2,1)}, f32[4096,1280]{1,0:T(8,128)}) fusion(f32[4096,1280]{1,0:T(8,128)} %fusion.47, bf16[1,512,1280]{2,1,0:T(8,128)(2,1)} %all-gather.15.cloned.1.call-done, bf16[1,4096,512]{1,2,0:T(8,128)(2,1)} %copy.20, f32[4096]{0:T(1024)S(1)} %add_rsqrt_fusion), kind=kOutput, calls=%fused_computation.17 | convolution fusion | flops 5406457856 | bytes 57950208 | tf_op jit(solution)/shard_map/dot_general | solution.py:22
  106.2 17.1 %all-gather.17.cloned.1.call-done = bf16[1,1280,512]{2,1,0:T(8,128)(2,1)} async-done(((bf16[1,80,512]{2,1,0:T(8,128)(2,1)}), bf16[1,1280,512]{2,1,0:T(8,128)(2,1)}) %all-gather.17.cloned.1.call-update) | async-done | bytes 1310736 | tf_op jit(solution)/shard_map/all_gather | solution.py:40
  123.3 11.2 %fusion.19 = (f32[4096]{0:T(1024)S(1)}, bf16[4096,512]{0,1:T(8,128)(2,1)}) fusion(bf16[4096,1280]{1,0:T(8,128)(2,1)} %get-tuple-element.24, bf16[1,1280,512]{2,1,0:T(8,128)(2,1)} %all-gather.17.cloned.1.call-done, bf16[1,4096,512]{1,2,0:T(8,128)(2,1)} %copy.20), kind=kOutput, calls=%fused_computation.37 | convolution fusion | flops 5379190784 | bytes 20201472 | tf_op jit(solution)/shard_map/dot_general | solution.py:10
  134.5 0.6 copy-done.14
  135.1 24.2 %all-gather.21.cloned.1.call-done = bf16[1,1280,512]{2,1,0:T(8,128)(2,1)} async-done(((bf16[1,80,512]{2,1,0:T(8,128)(2,1)}), bf16[1,1280,512]{2,1,0:T(8,128)(2,1)}) %all-gather.21.cloned.1.call-update) | async-done | bytes 1310736 | tf_op jit(solution)/shard_map/all_gather | solution.py:40
  159.4 10.5 %convolution_convert_fusion.1 = bf16[4096,1280]{1,0:T(8,128)(2,1)} fusion(bf16[1,4096,512]{2,1,0:T(8,128)(2,1)} %param.12, bf16[1,1280,512]{2,1,0:T(8,128)(2,1)} %all-gather.21.cloned.1.call-done), kind=kOutput, calls=%fused_computation.21 | convolution fusion | flops 5373952000 | bytes 15990784 | tf_op jit(solution)/shard_map/transpose(jvp())/dot_general | solution.py:10
  169.9 25.5 %all-gather.23.cloned.1.call-done = bf16[1,512,1280]{2,1,0:T(8,128)(2,1)} async-done(((bf16[1,32,1280]{2,1,0:T(8,128)(2,1)}), bf16[1,512,1280]{2,1,0:T(8,128)(2,1)}) %all-gather.23.cloned.1.call-update) | async-done | bytes 1310736 | tf_op jit(solution)/shard_map/all_gather | solution.py:40
  195.4 11.9 %fusion.39 = f32[4096,1280]{1,0:T(8,128)} fusion(bf16[4096,512]{0,1:T(8,128)(2,1)} %get-tuple-element.27, f32[4096]{0:T(1024)S(1)} %fusion.79, bf16[1,512,1280]{2,1,0:T(8,128)(2,1)} %all-gather.23.cloned.1.call-done), kind=kOutput, calls=%fused_computation.54 | convolution fusion | flops 5375000576 | bytes 26492928 | tf_op jit(solution)/shard_map/jvp()/dot_general | solution.py:22
  207.3 24.2 %all-gather.19.cloned.1.call-done = bf16[1,512,1280]{2,1,0:T(8,128)(2,1)} async-done(((bf16[1,32,1280]{2,1,0:T(8,128)(2,1)}), bf16[1,512,1280]{2,1,0:T(8,128)(2,1)}) %all-gather.19.cloned.1.call-update) | async-done | bytes 1310736 | tf_op jit(solution)/shard_map/all_gather | solution.py:40
  231.5 28.9 %fusion.2 = (bf16[4096,1280]{1,0:T(8,128)(2,1)}, f32[4096,1280]{1,0:T(8,128)}) fusion(f32[4096,1280]{1,0:T(8,128)} %fusion.39, bf16[4096,1280]{1,0:T(8,128)(2,1)} %convolution_convert_fusion.1, bf16[1,512,1280]{2,1,0:T(8,128)(2,1)} %all-gather.19.cloned.1.call-done, bf16[4096,512]{0,1:T(8,128)(2,1)} %get-tuple-element.27, f32[4096]{0:T(1024)S(1)} %fusion.79), kind=kOutput, calls=%fused_computation.8 | convolution fusion | flops 5437915136 | bytes 68435968 | tf_op jit(solution)/shard_map/jvp()/dot_general | solution.py:21
  260.4 9.6 %convolution_convert_fusion.4 = bf16[512,1280]{1,0:T(8,128)(2,1)} fusion(bf16[4096,1280]{1,0:T(8,128)(2,1)} %get-tuple-element.28, bf16[4096,512]{0,1:T(8,128)(2,1)S(1)} %copy-done.2, f32[4096]{0:T(1024)S(1)} %fusion.79), kind=kOutput, calls=%fused_computation.51 | convolution fusion | flops 5375000576 | bytes 16007168 | tf_op jit(solution)/shard_map/transpose(jvp())/dot_general | solution.py:21
  270.0 0.1 reduce-scatter.7.cloned.1.call-start
  270.1 15.5 %fusion.22 = bf16[4096,512]{0,1:T(8,128)(2,1)} fusion(bf16[4096,1280]{1,0:T(8,128)(2,1)} %convolution_convert_fusion.1, bf16[1,512,1280]{2,1,0:T(8,128)(2,1)S(1)} %copy-done.19, f32[4096,1280]{1,0:T(8,128)} %get-tuple-element.29), kind=kOutput, calls=%fused_computation.41 | convolution fusion | flops 5402263552 | bytes 36962304 | tf_op jit(solution)/shard_map/transpose(jvp())/dot_general | solution.py:22
  285.6 11.1 %fusion.21 = (f32[4096]{0:T(1024)S(1)}, bf16[4096,512]{0,1:T(8,128)(2,1)S(1)}) fusion(bf16[4096,512]{0,1:T(8,128)(2,1)S(1)} %copy-done.3, bf16[4096,512]{0,1:T(8,128)(2,1)} %fusion.22, bf16[4096,1280]{1,0:T(8,128)(2,1)} %get-tuple-element.28, bf16[1,512,1280]{2,1,0:T(8,128)(2,1)S(1)} %copy-done.20), kind=kOutput, calls=%fused_computation.39 | convolution fusion | flops 5379190784 | bytes 24395776 | tf_op jit(solution)/shard_map/transpose(jvp())/dot_general | solution.py:21
  296.9 2.8 fusion.25
  299.7 8.4 %convolution_convert_fusion = bf16[4096,1280]{1,0:T(8,128)(2,1)} fusion(bf16[4096,512]{0,1:T(8,128)(2,1)S(1)} %fusion.25, bf16[1,1280,512]{2,1,0:T(8,128)(2,1)S(1)} %copy-done.18), kind=kOutput, calls=%fused_computation.20 | convolution fusion | flops 5373952000 | bytes 15990784 | tf_op jit(solution)/shard_map/transpose(jvp())/dot_general | solution.py:10
  308.1 20.6 %fusion.32 = bf16[512,1280]{1,0:T(8,128)(2,1)} fusion(f32[4096,1280]{1,0:T(8,128)} %fusion.47, f32[4096,1280]{1,0:T(8,128)} %get-tuple-element.25, bf16[4096,1280]{1,0:T(8,128)(2,1)} %convolution_convert_fusion, bf16[1,4096,512]{1,2,0:T(8,128)(2,1)S(1)} %copy-done, f32[4096]{0:T(1024)S(1)} %copy-done.17), kind=kOutput, calls=%fused_computation.49 | convolution fusion | flops 5433327616 | bytes 57950208 | tf_op jit(solution)/shard_map/transpose(jvp())/dot_general | solution.py:21
  328.8 0.1 reduce-scatter.13.cloned.1.call-start
  328.9 16.3 %fusion.36 = bf16[512,1280]{1,0:T(8,128)(2,1)} fusion(bf16[4096,1280]{1,0:T(8,128)(2,1)} %convolution_convert_fusion.1, bf16[4096,512]{0,1:T(8,128)(2,1)} %get-tuple-element.27, f32[4096]{0:T(1024)S(1)} %fusion.79, f32[4096,1280]{1,0:T(8,128)} %get-tuple-element.29), kind=kOutput, calls=%fused_computation.52 | convolution fusion | flops 5407113216 | bytes 36978688 | tf_op jit(solution)/shard_map/transpose(jvp())/dot_general | solution.py:22
  345.3 16.3 %fusion.35 = bf16[512,1280]{1,0:T(8,128)(2,1)} fusion(bf16[4096,1280]{1,0:T(8,128)(2,1)} %convolution_convert_fusion, f32[4096,1280]{1,0:T(8,128)} %fusion.47, bf16[1,4096,512]{1,2,0:T(8,128)(2,1)} %copy.20, f32[4096]{0:T(1024)S(1)} %copy-done.17), kind=kOutput, calls=%fused_computation.50 | convolution fusion | flops 5407113216 | bytes 36978688 | tf_op jit(solution)/shard_map/transpose(jvp())/dot_general | solution.py:22
  361.7 0.1 reduce-scatter.17.cloned.1.call-start
  361.7 18.4 %fusion.29 = bf16[1280,512]{1,0:T(8,128)(2,1)} fusion(bf16[1,4096,512]{2,1,0:T(8,128)(2,1)} %param.12, f32[4096,1280]{1,0:T(8,128)} %fusion.39, f32[4096,1280]{1,0:T(8,128)} %get-tuple-element.29), kind=kOutput, calls=%fused_computation.48 | convolution fusion | flops 5400821760 | bytes 47448064 | tf_op jit(solution)/shard_map/transpose(jvp())/dot_general | solution.py:10
  380.3 0.1 reduce-scatter.15.cloned.1.call-start
  380.4 10.6 %convolution_convert_fusion.5 = bf16[1280,512]{1,0:T(8,128)(2,1)} fusion(bf16[4096,1280]{1,0:T(8,128)(2,1)} %get-tuple-element.24, bf16[4096,512]{0,1:T(8,128)(2,1)} %copy-done.4), kind=kOutput, calls=%fused_computation.53 | convolution fusion | flops 5369364480 | bytes 15990784 | tf_op jit(solution)/shard_map/transpose(jvp())/dot_general | solution.py:10
  391.2 1.6 fusion.67
  392.8 43.1 %reduce-scatter.13.cloned.1.call-done = bf16[32,1280]{1,0:T(8,128)(2,1)} async-done(((bf16[512,1280]{1,0:T(8,128)(2,1)}), bf16[32,1280]{1,0:T(8,128)(2,1)}) %reduce-scatter.13.cloned.1.call-update) | async-done | bytes 81936 | tf_op jit(solution)/shard_map/reduce_scatter | solution.py:53
  435.9 56.2 %reduce-scatter.11.cloned.1.call-done = bf16[32,1280]{1,0:T(8,128)(2,1)} async-done(((bf16[512,1280]{1,0:T(8,128)(2,1)}), bf16[32,1280]{1,0:T(8,128)(2,1)}) %reduce-scatter.11.cloned.1.call-update) | async-done | bytes 81936 | tf_op jit(solution)/shard_map/reduce_scatter | solution.py:53
  492.1 1.6 fusion.68
  495.0 53.5 %reduce-scatter.17.cloned.1.call-done = bf16[80,512]{1,0:T(8,128)(2,1)} async-done(((bf16[1280,512]{1,0:T(8,128)(2,1)}), bf16[80,512]{1,0:T(8,128)(2,1)}) %reduce-scatter.17.cloned.1.call-update) | async-done | bytes 81936 | tf_op jit(solution)/shard_map/reduce_scatter | solution.py:53
  548.4 56.2 %reduce-scatter.15.cloned.1.call-done = bf16[80,512]{1,0:T(8,128)(2,1)} async-done(((bf16[1280,512]{1,0:T(8,128)(2,1)}), bf16[80,512]{1,0:T(8,128)(2,1)}) %reduce-scatter.15.cloned.1.call-update) | async-done | bytes 81936 | tf_op jit(solution)/shard_map/reduce_scatter | solution.py:53
  604.6 1.6 fusion.69
  606.9 27.0 %psum.7 = f32[]{:T(128)} all-reduce(f32[]{:T(128)S(6)} %add.99), channel_id=1, replica_groups=mesh['rep'=4,'dp'=16] {'dp'}, use_global_device_ids=true, to_apply=%region_12.13 | all-reduce | flops 1 | bytes 8 | tf_op jit(solution)/shard_map/psum | solution.py:55
  634.7 1.9 fusion.75
  636.6 2.3 fusion.66
  (61 shorter events, 1.0 us)
Async XLA Ops:
  7.2 43.6 %all-gather.13.cloned.1.call-start = ((), (), s32[]{:S(2)}) async-start(), calls=%async_computation.12 | async-start | bytes 1392640 | tf_op jit(solution)/shard_map/all_gather | solution.py:40
  8.9 78.1 %all-gather.15.cloned.1.call-start = ((), (), s32[]{:S(2)}) async-start(), calls=%async_computation.13 | async-start | bytes 1392640 | tf_op jit(solution)/shard_map/all_gather | solution.py:40
  10.6 112.6 %all-gather.17.cloned.1.call-start = ((), (), s32[]{:S(2)}) async-start(), calls=%async_computation.14 | async-start | bytes 1392640 | tf_op jit(solution)/shard_map/all_gather | solution.py:40
  12.4 147.0 %all-gather.21.cloned.1.call-start = ((), (), s32[]{:S(2)}) async-start(), calls=%async_computation.16 | async-start | bytes 1392640 | tf_op jit(solution)/shard_map/all_gather | solution.py:40
  13.0 182.4 %all-gather.23.cloned.1.call-start = ((), (), s32[]{:S(2)}) async-start(), calls=%async_computation.17 | async-start | bytes 1392640 | tf_op jit(solution)/shard_map/all_gather | solution.py:40
  13.7 217.9 %all-gather.19.cloned.1.call-start = ((), (), s32[]{:S(2)}) async-start(), calls=%async_computation.15 | async-start | bytes 1392640 | tf_op jit(solution)/shard_map/all_gather | solution.py:40
  14.3 376.8 %reduce-scatter.9.cloned.1.call-start = ((), (), s32[]{:S(2)}) async-start(), calls=%async_computation.7 | async-start | bytes 1392640 | tf_op jit(solution)/shard_map/reduce_scatter | solution.py:53
  23.8 63.2 %copy-start.16 = (f32[4096]{0:T(1024)}, f32[4096]{0:T(1024)S(1)}, u32[]{:S(2)}) copy-start(f32[4096]{0:T(1024)S(1)} %add_rsqrt_fusion) | copy-start | bytes 49156
  134.5 0.6 copy-start.14
  231.5 28.9 %copy-start.2 = (bf16[4096,512]{0,1:T(8,128)(2,1)S(1)}, bf16[4096,512]{0,1:T(8,128)(2,1)}, u32[]{:S(2)}) copy-start(bf16[4096,512]{0,1:T(8,128)(2,1)} %get-tuple-element.27) | copy-start | bytes 12582916
  260.4 9.7 %copy-start.19 = (bf16[1,512,1280]{2,1,0:T(8,128)(2,1)S(1)}, bf16[1,512,1280]{2,1,0:T(8,128)(2,1)}, u32[]{:S(2)}) copy-start(bf16[1,512,1280]{2,1,0:T(8,128)(2,1)} %all-gather.23.cloned.1.call-done) | copy-start | bytes 3932164
  270.0 121.1 %reduce-scatter.7.cloned.1.call-start = ((), (), s32[]{:S(2)}) async-start(), calls=%async_computation.6 | async-start | bytes 1392640 | tf_op jit(solution)/shard_map/reduce_scatter | solution.py:53
  270.1 15.5 %copy-start.3 = (bf16[4096,512]{0,1:T(8,128)(2,1)S(1)}, bf16[4096,512]{0,1:T(8,128)(2,1)}, u32[]{:S(2)}) copy-start(bf16[4096,512]{0,1:T(8,128)(2,1)} %get-tuple-element.27) | copy-start | bytes 12582916
  270.1 15.5 %copy-start.20 = (bf16[1,512,1280]{2,1,0:T(8,128)(2,1)S(1)}, bf16[1,512,1280]{2,1,0:T(8,128)(2,1)}, u32[]{:S(2)}) copy-start(bf16[1,512,1280]{2,1,0:T(8,128)(2,1)} %all-gather.19.cloned.1.call-done) | copy-start | bytes 3932164
  285.6 11.2 %copy-start.15 = (f32[4096]{0:T(1024)S(1)}, f32[4096]{0:T(1024)}, u32[]{:S(2)}) copy-start(f32[4096]{0:T(1024)} %copy-done.14) | copy-start | bytes 49156
  285.6 11.2 %copy-start.1 = (bf16[1,4096,512]{1,2,0:T(8,128)(2,1)S(1)}, bf16[1,4096,512]{1,2,0:T(8,128)(2,1)}, u32[]{:S(2)}) copy-start(bf16[1,4096,512]{1,2,0:T(8,128)(2,1)} %copy.21) | copy-start | bytes 12582916
  296.8 2.8 copy-start.18
  299.7 8.4 %copy-start.4 = (bf16[4096,512]{0,1:T(8,128)(2,1)}, bf16[4096,512]{0,1:T(8,128)(2,1)S(1)}, u32[]{:S(2)}) copy-start(bf16[4096,512]{0,1:T(8,128)(2,1)S(1)} %fusion.25) | copy-start | bytes 12582916
  299.7 8.4 %copy-start = (bf16[1,4096,512]{1,2,0:T(8,128)(2,1)S(1)}, bf16[1,4096,512]{1,2,0:T(8,128)(2,1)}, u32[]{:S(2)}) copy-start(bf16[1,4096,512]{1,2,0:T(8,128)(2,1)} %copy.20) | copy-start | bytes 12582916
  299.7 8.4 %copy-start.17 = (f32[4096]{0:T(1024)S(1)}, f32[4096]{0:T(1024)}, u32[]{:S(2)}) copy-start(f32[4096]{0:T(1024)} %copy-done.16) | copy-start | bytes 49156
  328.8 107.1 %reduce-scatter.13.cloned.1.call-start = ((), (), s32[]{:S(2)}) async-start(), calls=%async_computation.9 | async-start | bytes 1392640 | tf_op jit(solution)/shard_map/reduce_scatter | solution.py:53
  345.2 146.8 %reduce-scatter.11.cloned.1.call-start = ((), (), s32[]{:S(2)}) async-start(), calls=%async_computation.8 | async-start | bytes 1392640 | tf_op jit(solution)/shard_map/reduce_scatter | solution.py:53
  361.7 186.8 %reduce-scatter.17.cloned.1.call-start = ((), (), s32[]{:S(2)}) async-start(), calls=%async_computation.11 | async-start | bytes 1392640 | tf_op jit(solution)/shard_map/reduce_scatter | solution.py:53
  380.2 254.4 %copy-start.5 = (bf16[2,80,512]{2,1,0:T(8,128)(2,1)S(1)}, bf16[2,80,512]{2,1,0:T(8,128)(2,1)}, u32[]{:S(2)}) copy-start(bf16[2,80,512]{2,1,0:T(8,128)(2,1)} %param.15) | copy-start | bytes 491524
  380.2 254.4 %copy-start.8 = (f32[2,80,512]{2,1,0:T(8,128)S(1)}, f32[2,80,512]{2,1,0:T(8,128)}, u32[]{:S(2)}) copy-start(f32[2,80,512]{2,1,0:T(8,128)} %param.21) | copy-start | bytes 983044
  380.3 254.4 %copy-start.9 = (f32[2,80,512]{2,1,0:T(8,128)S(1)}, f32[2,80,512]{2,1,0:T(8,128)}, u32[]{:S(2)}) copy-start(f32[2,80,512]{2,1,0:T(8,128)} %param.18) | copy-start | bytes 983044
  380.3 256.3 %copy-start.6 = (bf16[2,32,1280]{2,1,0:T(8,128)(2,1)S(1)}, bf16[2,32,1280]{2,1,0:T(8,128)(2,1)}, u32[]{:S(2)}) copy-start(bf16[2,32,1280]{2,1,0:T(8,128)(2,1)} %param.13) | copy-start | bytes 491524
  380.3 256.3 %copy-start.7 = (bf16[2,32,1280]{2,1,0:T(8,128)(2,1)S(1)}, bf16[2,32,1280]{2,1,0:T(8,128)(2,1)}, u32[]{:S(2)}) copy-start(bf16[2,32,1280]{2,1,0:T(8,128)(2,1)} %param.14) | copy-start | bytes 491524
  380.3 256.3 %copy-start.10 = (f32[2,32,1280]{2,1,0:T(8,128)S(1)}, f32[2,32,1280]{2,1,0:T(8,128)}, u32[]{:S(2)}) copy-start(f32[2,32,1280]{2,1,0:T(8,128)} %param.19) | copy-start | bytes 983044
  380.3 256.3 %copy-start.11 = (f32[2,32,1280]{2,1,0:T(8,128)S(1)}, f32[2,32,1280]{2,1,0:T(8,128)}, u32[]{:S(2)}) copy-start(f32[2,32,1280]{2,1,0:T(8,128)} %param.16) | copy-start | bytes 983044
  380.3 256.3 %copy-start.12 = (f32[2,32,1280]{2,1,0:T(8,128)S(1)}, f32[2,32,1280]{2,1,0:T(8,128)}, u32[]{:S(2)}) copy-start(f32[2,32,1280]{2,1,0:T(8,128)} %param.20) | copy-start | bytes 983044
  380.3 256.3 %copy-start.13 = (f32[2,32,1280]{2,1,0:T(8,128)S(1)}, f32[2,32,1280]{2,1,0:T(8,128)}, u32[]{:S(2)}) copy-start(f32[2,32,1280]{2,1,0:T(8,128)} %param.17) | copy-start | bytes 983044
  380.3 224.3 %reduce-scatter.15.cloned.1.call-start = ((), (), s32[]{:S(2)}) async-start(), calls=%async_computation.10 | async-start | bytes 1392640 | tf_op jit(solution)/shard_map/reduce_scatter | solution.py:53
Sparse Core Ops, SparseCore 0:
  10.2 40.5 all-gather.12
  53.0 33.9 all-gather.14
  89.2 33.9 all-gather.16
  125.3 33.9 all-gather.20
  161.4 33.9 all-gather.22
  197.5 33.9 all-gather.18
  270.2 50.5 reduce-scatter.8
  328.9 50.5 reduce-scatter.6
  381.9 53.9 reduce-scatter.12
  438.0 53.9 reduce-scatter.10
  494.4 54.0 reduce-scatter.16
  550.6 53.9 reduce-scatter.14
where the time goes:
time: 656 us; the launch traced here: 646 us
  waiting for transfers between devices  347 us (53%)
  matrix products  220 us (34%)
  blocking collectives  27 us (4%)
  local copies, waits for them, and re-layouts  18.3 us (3%)
  between operations  17.6 us (3%)
  other arithmetic  15 us (2%)
    reduce_scatter x6, waiting for transfers between devices, step(): lax.psum_scatter(by_w[name], 'dp', scatter_dimension=0, tiled=True)  209 us
    all_gather x6, waiting for transfers between devices, fetched(): lax.all_gather(w[number], 'dp', axis=0, tiled=True)  136 us
    dot_general x5, matrix products, layer(): gate = jnp.dot(a, w['w_gate'], preferred_element_type=jnp.float32)  82.1 us
    dot_general x5, matrix products, layer(): up = jnp.dot(a, w['w_up'], preferred_element_type=jnp.float32)  79.1 us
    dot_general x5, matrix products, matmul(): jnp.dot(a, w, preferred_element_type=jnp.float32).astype(jnp.bfloat16)  59.2 us
    psum x1, blocking collectives, step(): squares = lax.psum(sum((jnp.sum(g * g) for g in gradients)), 'dp')  27 us
    unnamed x44, local copies, waits for them, and re-layouts  13.5 us
  transfers between devices with their start and end apart: 12, of which 10 were waited for; matrix products, arithmetic and copies ran while one was open for 32% of the time, Pallas kernels for 0%

commit v1 on v0

v1 whole, which is shorter than its diff:
```python
import functools

import jax
import jax.numpy as jnp
from jax import lax
from jax.experimental import pallas as pl
from jax.experimental.pallas import tpu as pltpu
from jax.sharding import PartitionSpec as P

MESH = pl.DeviceIdType.MESH
BF, F32 = jnp.bfloat16, jnp.float32
VMEM_LIMIT = 66_500_000
TILE = 512
WIDE = 1024
COLS = 256


def dot(a, b):
    return jnp.dot(a, b, preferred_element_type=F32)


def dot_t(a, b):
    return lax.dot_general(a, b, (((0,), (0,)), ((), ())), preferred_element_type=F32)


def norm_scale(wide):
    return lax.rsqrt(jnp.mean(wide * wide, -1, keepdims=True) + 1e-6)


def places(n):
    nz = n // 2
    me = lax.axis_index("dp")
    z, core = me // 2, me % 2
    return me, z, core, ((z + 1) % nz) * 2 + core, ((z + nz - 1) % nz) * 2 + core, me + 1 - 2 * core


def barrier(devices):
    sem = pltpu.get_barrier_semaphore()
    for device in devices:
        pl.semaphore_signal(sem, inc=1, device_id={"dp": device}, device_id_type=MESH)
    pl.semaphore_wait(sem, len(devices))


def forward_kernel(n, x_hbm, wg_ref, wu_ref, wd_ref, h1_hbm, hid_hbm, a0_hbm, gu_hbm, d_hbm, dt_hbm,
                   x, a0, hid, gu, d, dt, send_sem, recv_sem, in_sem, out_sem):
    nz = n // 2
    me, z, core, right, left, partner = places(n)
    tokens = x.shape[0]
    steps = tokens // TILE
    load = pltpu.make_async_copy(x_hbm, x, in_sem)
    load.start()
    barrier((right, left, partner))

    more, less = nz // 2, nz - 1 - nz // 2
    parts = [
        (wg_ref.at[0], gu, 0, more, less),
        (wu_ref.at[0], gu, 1, less, more),
        (wd_ref.at[0], d, 0, more, less),
        (wg_ref.at[1], gu, 2, less, more),
        (wu_ref.at[1], gu, 3, more, less),
        (wd_ref.at[1], d, 1, less, more),
    ]
    sent = []

    def block(i, chip, which):
        src, whole, first, _, _ = parts[i]
        rows = src.shape[0]
        at = pl.multiple_of((chip * 2 + which) * rows, 16)
        return whole.at[first, pl.ds(at, rows), :]

    def copy(i, k, src, dst, device):
        return pltpu.make_async_remote_copy(
            src_ref=src, dst_ref=dst, send_sem=send_sem.at[i, k], recv_sem=recv_sem.at[i, k],
            device_id={"dp": device}, device_id_type=MESH,
        )

    def send(i, k, src, dst, device):
        c = copy(i, k, src, dst, device)
        c.start()
        sent.append(c)

    def arrived(i, k, at):
        copy(i, k, at, at, partner).wait_recv()

    def begin(i):
        src = parts[i][0]
        own = block(i, z, core)
        send(i, 0, src, own, right)
        send(i, more, src, own, left)
        send(i, 2 * more, src, own, partner)
        rows = src.shape[0]
        whole, first = parts[i][1], parts[i][2]
        whole[first, pl.ds(pl.multiple_of(me * rows, 16), rows), :] = src[...]

    def relay(i, s):
        _, _, _, hops_right, hops_left = parts[i]
        if s <= hops_right:
            at = block(i, (z + nz - s) % nz, core)
            arrived(i, s - 1, at)
            if s < hops_right:
                send(i, s, at, at, right)
            send(i, 2 * more + s, at, at, partner)
        if s <= hops_left:
            at = block(i, (z + s) % nz, core)
            arrived(i, more + s - 1, at)
            if s < hops_left:
                send(i, more + s, at, at, left)
            send(i, 3 * more + s, at, at, partner)

    def finish(i):
        _, _, _, hops_right, hops_left = parts[i]
        arrived(i, 2 * more, block(i, z, 1 - core))
        for s in range(1, hops_right + 1):
            arrived(i, 2 * more + s, block(i, (z + nz - s) % nz, 1 - core))
        for s in range(1, hops_left + 1):
            arrived(i, 3 * more + s, block(i, (z + s) % nz, 1 - core))

    outs = []

    def store(k, src, dst):
        c = pltpu.make_async_copy(src, dst, out_sem.at[k])
        c.start()
        outs.append(c)

    begin(0)
    begin(1)
    load.wait()

    def norm_step(t, _):
        at = pl.ds(pl.multiple_of(t * TILE, TILE), TILE)
        wide = x[at, :].astype(F32)
        a0[at, :] = (wide * norm_scale(wide)).astype(BF)
        return 0

    relay(0, 1)
    relay(1, 1)
    lax.fori_loop(0, steps // 2, norm_step, 0)
    relay(0, 2)
    relay(1, 2)
    lax.fori_loop(steps // 2, steps, norm_step, 0)
    for s in range(3, more + 1):
        relay(0, s)
        relay(1, s)
    begin(2)
    begin(3)
    finish(0)
    finish(1)
    store(0, a0, a0_hbm)

    def up_step(t, _):
        at = pl.ds(pl.multiple_of(t * TILE, TILE), TILE)
        a = a0[at, :]
        gate = dot(a, gu[0])
        up = dot(a, gu[1])
        hid[at, :] = (gate * jax.nn.sigmoid(gate) * up).astype(BF)
        return 0

    def down_step(t, _):
        at = pl.ds(pl.multiple_of(t * TILE, TILE), TILE)
        x[at, :] = x[at, :] + dot(hid[at, :], d[0]).astype(BF)
        return 0

    quarter = steps // 4
    for q in range(4):
        lax.fori_loop(q * quarter, (q + 1) * quarter, up_step, 0)
        s = q + 1
        if s <= more:
            relay(2, s)
            relay(3, s)
        if s == 3:
            begin(4)
            begin(5)
    for s in range(5, more + 1):
        relay(2, s)
        relay(3, s)
    store(1, hid, hid_hbm)
    relay(4, 1)
    relay(5, 1)
    finish(2)
    dt[...] = d[0].T
    store(2, dt, dt_hbm)
    for q in range(4):
        lax.fori_loop(q * quarter, (q + 1) * quarter, down_step, 0)
        if q == 1:
            relay(4, 2)
            relay(5, 2)
    store(3, x, h1_hbm)
    for s in range(3, more + 1):
        relay(4, s)
        relay(5, s)
    finish(3)
    finish(4)
    finish(5)
    store(4, gu, gu_hbm)
    store(5, d, d_hbm)
    for c in sent:
        c.wait_send()
    for c in outs:
        c.wait()


def forward(n, x, wg, wu, wd):
    tokens, dim = x.shape
    hidden = wg.shape[2]
    anyspace, vmem = pl.BlockSpec(memory_space=pl.ANY), pl.BlockSpec(memory_space=pltpu.VMEM)
    shapes = [(tokens, dim), (tokens, hidden), (tokens, dim), (4, dim, hidden), (2, hidden, dim), (dim, hidden)]
    sems = 4 * (n // 4) + 1
    return pl.pallas_call(
        functools.partial(forward_kernel, n),
        out_shape=[jax.ShapeDtypeStruct(s, BF) for s in shapes],
        in_specs=[anyspace, vmem, vmem, vmem],
        out_specs=[anyspace] * 6,
        scratch_shapes=[
            pltpu.VMEM((tokens, dim), BF),
            pltpu.VMEM((tokens, dim), BF),
            pltpu.VMEM((tokens, hidden), BF),
            pltpu.VMEM((4, dim, hidden), BF),
            pltpu.VMEM((2, hidden, dim), BF),
            pltpu.VMEM((dim, hidden), BF),
            pltpu.SemaphoreType.DMA((6, sems)),
            pltpu.SemaphoreType.DMA((6, sems)),
            pltpu.SemaphoreType.DMA,
            pltpu.SemaphoreType.DMA((6,)),
        ],
        compiler_params=pltpu.CompilerParams(collective_id=0, has_side_effects=True, vmem_limit_bytes=VMEM_LIMIT),
        cost_estimate=pl.CostEstimate(flops=6 * tokens * dim * hidden, bytes_accessed=40 << 20, transcendentals=0),
        name="forward0",
    )(x, wg, wu, wd)


def top_kernel(h1, dy, gu, d, dh, dgu, dd, gt, ut, dt, acc_g, acc_u, acc_d):
    t = pl.program_id(0)

    @pl.when(t == 0)
    def _():
        gt[...] = gu[0].T
        ut[...] = gu[1].T
        dt[...] = d[0].T
        acc_g[...] = jnp.zeros_like(acc_g)
        acc_u[...] = jnp.zeros_like(acc_u)
        acc_d[...] = jnp.zeros_like(acc_d)

    wide = h1[...].astype(F32)
    scale = norm_scale(wide)
    a = (wide * scale).astype(BF)
    by_y = dy[...]
    gate = dot(a, gu[0])
    up = dot(a, gu[1])
    by_hid = dot(by_y, dt[...]).astype(BF).astype(F32)
    sig = jax.nn.sigmoid(gate)
    act = gate * sig
    hid = (act * up).astype(BF)
    by_up = (by_hid * act).astype(BF)
    by_gate = (by_hid * up * (sig + act * (1.0 - sig))).astype(BF)
    acc_d[...] += dot_t(hid, by_y)
    acc_g[...] += dot_t(a, by_gate)
    acc_u[...] += dot_t(a, by_up)
    by_a = (dot(by_gate, gt[...]).astype(BF) + dot(by_up, ut[...]).astype(BF)).astype(F32)
    wide = h1[...].astype(F32)
    by_h = scale * by_a - wide * (scale * scale * scale * jnp.mean(by_a * wide, -1, keepdims=True))
    dh[...] = by_y + by_h.astype(BF)

    @pl.when(t == pl.num_programs(0) - 1)
    def _():
        dgu[0] = acc_g[...].astype(BF)
        dgu[1] = acc_u[...].astype(BF)
        dd[...] = acc_d[...].astype(BF)


def top(h1, dy, gu, d):
    tokens, dim = h1.shape
    hidden = gu.shape[2]
    tile = pl.BlockSpec((TILE, dim), lambda t: (t, 0))
    once = pl.Buffered(1)
    return pl.pallas_call(
        top_kernel,
        grid=(tokens // TILE,),
        out_shape=[
            jax.ShapeDtypeStruct((tokens, dim), BF),
            jax.ShapeDtypeStruct((2, dim, hidden), BF),
            jax.ShapeDtypeStruct((hidden, dim), BF),
        ],
        in_specs=[
            tile,
            tile,
            pl.BlockSpec((2, dim, hidden), lambda t: (1, 0, 0), pipeline_mode=once),
            pl.BlockSpec((1, hidden, dim), lambda t: (1, 0, 0), pipeline_mode=once),
        ],
        out_specs=[
            tile,
            pl.BlockSpec((2, dim, hidden), lambda t: (0, 0, 0), pipeline_mode=once),
            pl.BlockSpec((hidden, dim), lambda t: (0, 0), pipeline_mode=once),
        ],
        scratch_shapes=[
            pltpu.VMEM((hidden, dim), BF),
            pltpu.VMEM((hidden, dim), BF),
            pltpu.VMEM((dim, hidden), BF),
            pltpu.VMEM((dim, hidden), F32),
            pltpu.VMEM((dim, hidden), F32),
            pltpu.VMEM((hidden, dim), F32),
        ],
        compiler_params=pltpu.CompilerParams(vmem_limit_bytes=VMEM_LIMIT),
        cost_estimate=pl.CostEstimate(flops=16 * tokens * dim * hidden, bytes_accessed=24 << 20, transcendentals=0),
        name="layer1",
    )(h1, dy, gu, d)


def backward_kernel(n, a0_hbm, hid_hbm, dh_hbm, gu_hbm, dt_hbm, tgu_hbm, td_hbm, sum_gu, sum_d, squares,
                    a0, hid, dh, gu, dt, tgu1, td1, tgu0, td0, acc_g, acc_u, acc_d,
                    pgu1, pd1, pgu0, pd0, sgu1, sd1, sgu0, sd0, rgu1, rd1, rgu0, rd0, ssq, all_ssq,
                    in_sem, p_send, p_recv, send1, recv1, send0, recv0, q_send, q_recv):
    nz = n // 2
    me, z, core, right, left, partner = places(n)
    tokens, dim = a0.shape
    hidden = dt.shape[1]
    nf = hidden // COLS
    last = nz - 1
    rows_g, rows_d = dim // n, hidden // n

    def load(k, src, dst):
        c = pltpu.make_async_copy(src, dst, in_sem.at[k])
        c.start()
        return c

    first = [load(0, tgu_hbm, tgu1), load(1, td_hbm, td1)]
    half_t = tokens // 2
    second = [load(2, hid_hbm.at[pl.ds(0, half_t), :], hid.at[pl.ds(0, half_t), :]), load(3, dh_hbm, dh)]
    third = [load(4, hid_hbm.at[pl.ds(half_t, half_t), :], hid.at[pl.ds(half_t, half_t), :])]
    fourth = [load(5, a0_hbm, a0), load(6, gu_hbm.at[pl.ds(0, 2)], gu), load(7, dt_hbm, dt)]

    sem = pltpu.get_barrier_semaphore()
    for k in range(1, n):
        pl.semaphore_signal(sem, inc=1, device_id={"dp": (me + k) % n}, device_id_type=MESH)
    pl.semaphore_wait(sem, n - 1)

    def over(k, src, dst):
        return pltpu.make_async_remote_copy(
            src_ref=src, dst_ref=dst, send_sem=p_send.at[k], recv_sem=p_recv.at[k],
            device_id={"dp": partner}, device_id_type=MESH,
        )

    over_gu1 = over(nf, tgu1.at[:, :, 1 - core], pgu1)
    over_d1 = over(nf + 1, td1.at[:, 1 - core], pd1)
    over_d0 = over(nf + 2, td0.at[:, 1 - core], pd0)

    def over_gu0(j):
        return over(j, tgu0.at[j, :, :, 1 - core], pgu0.at[j])

    for c in first:
        c.wait()
    over_gu1.start()
    over_d1.start()
    ssq[...] = jnp.zeros_like(ssq)

    def move(send_ref, recv_ref, send_s, recv_s, device):
        return pltpu.make_async_remote_copy(
            src_ref=send_ref, dst_ref=recv_ref, send_sem=send_s, recv_sem=recv_s, device_id={"dp": device}, device_id_type=MESH
        )

    def squared(v):
        g = v.astype(F32)
        g = g * g
        while g.ndim > 2:
            g = jnp.sum(g, axis=0)
        g = jnp.sum(g, axis=0, keepdims=True)
        total = g[:, 0:128]
        for k in range(1, g.shape[1] // 128):
            total = total + g[:, k * 128 : (k + 1) * 128]
        ssq[0:1, :] += total

    def event(parts, s):
        def chip(way):
            return (z + 2 * nz - 1 - s) % nz if way == 0 else (z + 1 + s) % nz

        def term(part, way, b):
            width = part["width"]
            at = slice(way * width, (way + 1) * width)
            return part["own"](b, at).astype(F32) + part["other"](b, at).astype(F32)

        def wait(part, way):
            part["move"](way, s - 1).wait_recv()

        def go(part, way):
            part["move"](way, s).start()

        @pl.when(s == 0)
        def _():
            for way in range(2):
                for part in parts:
                    part["send"][way, s] = term(part, way, chip(way)).astype(BF)
            for way in range(2):
                for part in parts:
                    go(part, way)

        @pl.when(jnp.logical_and(s > 0, s < last))
        def _():
            for way in range(2):
                for part in parts:
                    wait(part, way)
                    v = part["recv"][way, s - 1].astype(F32) + term(part, way, chip(way))
                    part["send"][way, s] = v.astype(BF)
                for part in parts:
                    go(part, way)

        @pl.when(s == last)
        def _():
            for way in range(2):
                for part in parts:
                    wait(part, way)
                    v = (part["recv"][way, s - 1].astype(F32) + term(part, way, chip(way))).astype(BF)
                    part["put"](way, v)
                    squared(v)

    class Slots:
        def __init__(self, ref, *lead):
            self.ref, self.lead = ref, lead

        def __getitem__(self, k):
            return self.ref[self.lead + k]

        def __setitem__(self, k, v):
            self.ref[self.lead + k] = v

    def part(width, own, other, s_ref, r_ref, sems, k, lead, put):
        def the_move(way, s):
            return move(s_ref.at[lead + (way, s)], r_ref.at[lead + (way, s)], sems[0].at[k, way, s], sems[1].at[k, way, s], right if way == 0 else left)

        return dict(width=width, own=own, other=other, send=Slots(s_ref, *lead), recv=Slots(r_ref, *lead), move=the_move, put=put)

    def put_gu1(way, v):
        w = hidden // 2
        sum_gu[1, :, :, way * w : (way + 1) * w] = v

    def put_d(layer):
        def put(way, v):
            w = dim // 2
            sum_d[layer, :, way * w : (way + 1) * w] = v

        return put

    gu1 = part(hidden // 2, lambda b, at: tgu1[:, b, core, :, at], lambda b, at: pgu1[:, b, :, at], sgu1, rgu1, (send1, recv1), 0, (), put_gu1)
    d1 = part(dim // 2, lambda b, at: td1[b, core, :, at], lambda b, at: pd1[b, :, at], sd1, rd1, (send1, recv1), 1, (), put_d(1))
    d0 = part(dim // 2, lambda b, at: td0[b, core, :, at], lambda b, at: pd0[b, :, at], sd0, rd0, (send1, recv1), 2, (), put_d(0))

    def gu0(j):
        def put(way, v):
            w = COLS // 2
            sum_gu[0, :, :, pl.ds(pl.multiple_of(j * COLS + way * w, w), w)] = v

        return part(COLS // 2, lambda b, at: tgu0[j, :, b, core, :, at], lambda b, at: pgu0[j, :, b, :, at], sgu0, rgu0, (send0, recv0), j, (j,), put)

    for c in second:
        c.wait()
    acc_d[...] = jnp.zeros_like(acc_d)

    def down_step(t, _):
        at = pl.ds(pl.multiple_of(t * TILE, TILE), TILE)
        acc_d[...] += dot_t(hid[at, :], dh[at, :])
        return 0

    steps = tokens // TILE
    lax.fori_loop(0, steps // 2, down_step, 0)
    over_gu1.wait_recv()
    over_d1.wait_recv()
    event((gu1, d1), jnp.int32(0))
    third[0].wait()
    lax.fori_loop(steps // 2, steps, down_step, 0)
    for b in range(nz):
        for c in range(2):
            k = (b * 2 + c) * rows_d
            td0[b, c] = acc_d[k : k + rows_d, :].astype(BF)
    over_d0.start()
    for c in fourth:
        c.wait()

    half = tokens // WIDE // 2

    def wide_step(j):
        cols = pl.ds(pl.multiple_of(j * COLS, COLS), COLS)

        def body(t, _):
            at = pl.ds(pl.multiple_of(t * WIDE, WIDE), WIDE)
            a = a0[at, :]
            gate = dot(a, gu[0, :, cols])
            up = dot(a, gu[1, :, cols])
            by_hid = dot(dh[at, :], dt[:, cols]).astype(BF).astype(F32)
            sig = jax.nn.sigmoid(gate)
            act = gate * sig
            by_up = (by_hid * act).astype(BF)
            by_gate = (by_hid * up * (sig + act * (1.0 - sig))).astype(BF)
            acc_g[...] += dot_t(a, by_gate)
            acc_u[...] += dot_t(a, by_up)
            return 0

        return body

    def events(p, compute):
        @pl.when(p + 1 <= last)
        def _():
            event((gu1, d1), p + 1)

        @pl.when(p == 0)
        def _():
            over_d0.wait_recv()

        @pl.when(p <= last)
        def _():
            event((d0,), p)

        def each(j, _):
            s = p - (2 * j + 2)

            @pl.when(s == 0)
            def _():
                over_gu0(j).wait_recv()

            @pl.when(jnp.logical_and(s >= 0, s <= last))
            def _():
                event((gu0(j),), s)

            return 0

        lax.fori_loop(0, nf, each, 0)

    def phase(p, _):
        j, part_of = p // 2, p % 2

        @pl.when(part_of == 0)
        def _():
            acc_g[...] = jnp.zeros_like(acc_g)
            acc_u[...] = jnp.zeros_like(acc_u)

        lax.fori_loop(part_of * half, part_of * half + half, wide_step(j), 0)

        @pl.when(part_of == 1)
        def _():
            for b in range(nz):
                for c in range(2):
                    k = (b * 2 + c) * rows_g
                    tgu0[j, 0, b, c] = acc_g[k : k + rows_g, :].astype(BF)
                    tgu0[j, 1, b, c] = acc_u[k : k + rows_g, :].astype(BF)
            over_gu0(j).start()

        events(p, True)
        return 0

    def tail(p, _):
        events(p, False)
        return 0

    lax.fori_loop(0, 2 * nf, phase, 0)
    lax.fori_loop(2 * nf, 2 * nf + nz, tail, 0)

    all_ssq[me] = ssq[...]

    def scalar(k):
        return pltpu.make_async_remote_copy(
            src_ref=ssq, dst_ref=all_ssq.at[me], send_sem=q_send.at[k], recv_sem=q_recv.at[k],
            device_id={"dp": (me + k) % n}, device_id_type=MESH,
        )

    def tell(k, _):
        scalar(k).start()
        return 0

    lax.fori_loop(1, n, tell, 0)

    for c in (over_gu1, over_d1, over_d0):
        c.wait_send()

    def left_over(j, _):
        over_gu0(j).wait_send()
        for way in range(2):
            def one(s, _):
                gu0(j)["move"](way, s).wait_send()
                return 0
            lax.fori_loop(0, last, one, 0)
        return 0

    lax.fori_loop(0, nf, left_over, 0)

    def left_one(s, _):
        for way in range(2):
            for q in (gu1, d1, d0):
                q["move"](way, s).wait_send()
        return 0

    lax.fori_loop(0, last, left_one, 0)

    def told(k, _):
        src = (me + n - k) % n
        pltpu.make_async_remote_copy(
            src_ref=ssq, dst_ref=all_ssq.at[src], send_sem=q_send.at[k], recv_sem=q_recv.at[k],
            device_id={"dp": (me + k) % n}, device_id_type=MESH,
        ).wait()
        return 0

    lax.fori_loop(1, n, told, 0)
    squares[...] = jnp.sum(all_ssq[...], axis=0)


def backward(n, a0, hid, dh, gu, dt, tgu, td):
    nz = n // 2
    tokens, dim = a0.shape
    hidden = dt.shape[1]
    nf, last = hidden // COLS, nz - 1
    rg, rd = dim // n, hidden // n
    anyspace, vmem = pl.BlockSpec(memory_space=pl.ANY), pl.BlockSpec(memory_space=pltpu.VMEM)
    V = lambda *s: pltpu.VMEM(s, BF)
    S = lambda *s: pltpu.SemaphoreType.DMA(s)
    slots = [
        V(2, last, 2, rg, hidden // 2),
        V(2, last, rd, dim // 2),
        V(nf, 2, last, 2, rg, COLS // 2),
        V(2, last, rd, dim // 2),
    ]
    return pl.pallas_call(
        functools.partial(backward_kernel, n),
        out_shape=[
            jax.ShapeDtypeStruct((2, 2, rg, hidden), BF),
            jax.ShapeDtypeStruct((2, rd, dim), BF),
            jax.ShapeDtypeStruct((8, 128), F32),
        ],
        in_specs=[anyspace] * 7,
        out_specs=[vmem] * 3,
        scratch_shapes=[
            V(tokens, dim),
            V(tokens, hidden),
            V(tokens, dim),
            V(2, dim, hidden),
            V(dim, hidden),
            V(2, nz, 2, rg, hidden),
            V(nz, 2, rd, dim),
            V(nf, 2, nz, 2, rg, COLS),
            V(nz, 2, rd, dim),
            pltpu.VMEM((dim, COLS), F32),
            pltpu.VMEM((dim, COLS), F32),
            pltpu.VMEM((hidden, dim), F32),
            V(2, nz, rg, hidden),
            V(nz, rd, dim),
            V(nf, 2, nz, rg, COLS),
            V(nz, rd, dim),
            *slots,
            *slots,
            pltpu.VMEM((8, 128), F32),
            pltpu.VMEM((n, 8, 128), F32),
            S(8),
            S(nf + 3),
            S(nf + 3),
            S(3, 2, last),
            S(3, 2, last),
            S(nf, 2, last),
            S(nf, 2, last),
            S(n),
            S(n),
        ],
        compiler_params=pltpu.CompilerParams(collective_id=1, has_side_effects=True, vmem_limit_bytes=VMEM_LIMIT),
        cost_estimate=pl.CostEstimate(flops=12 * tokens * dim * hidden, bytes_accessed=40 << 20, transcendentals=0),
        name="backward0",
    )(a0, hid, dh, gu, dt, tgu.reshape(2, nz, 2, rg, hidden), td.reshape(nz, 2, rd, dim))


def adamw(w, m, v, g):
    m = 0.9 * m + 0.1 * g
    v = 0.95 * v + 0.05 * g * g
    step = m * lax.rsqrt(v + 1e-8) + 0.1 * w
    return (w - 0.02 * step).astype(BF), m, v


def solution(mesh):
    n = mesh.shape["dp"]

    def step(x, dy, *arrays):
        weights, m, v = (arrays[i : i + 3] for i in (0, 3, 6))
        h1, hid, a0, gu, d, dt = forward(n, x[0], *weights)
        dh, tgu, td = top(h1, dy[0], gu, d)
        sum_gu, sum_d, squares = backward(n, a0, hid, dh, gu, dt, tgu, td)
        gradients = [sum_gu[:, 0].astype(F32), sum_gu[:, 1].astype(F32), sum_d.astype(F32)]
        count = n * sum(g.size for g in gradients)
        factor = jnp.minimum(1.0, 0.5 * lax.rsqrt(jnp.sum(squares) / count + 1e-30))
        new = [adamw(w.astype(F32), m, v, g * factor) for w, m, v, g in zip(weights, m, v, gradients, strict=True)]
        return tuple(one[which] for which in range(3) for one in new)

    states, cut = P(("rep", "dp"), None, None), P(None, "dp", None)
    return jax.shard_map(
        step,
        mesh=mesh,
        in_specs=(states, states) + (cut,) * 9,
        out_specs=(P("rep", "dp", None),) * 9,
        check_vma=False,
    )
```

time: 656 us -> 229 us (0.35); the launches traced: 646 us -> 229 us
  waiting for transfers between devices: 347 us -> 0 us
  Pallas kernels: 0 us -> 221 us
  matrix products: 220 us -> 0 us
  blocking collectives: 27 us -> 0 us
  local copies, waits for them, and re-layouts: 18.3 us -> 0.01 us
  between operations: 17.6 us -> 1.38 us
  other arithmetic: 15 us -> 6.12 us
    pallas_call x0 -> x3, Pallas kernels: none -> 221 us  [the longest x1 93.2 us: backward(): pl.pallas_call(functools.partial(backward_kernel, n), out_shape=[jax.Shap...]
    dot_general x15 -> x0, matrix products: 220 us -> none  [the longest x5 82.1 us: layer(): gate = jnp.dot(a, w['w_gate'], preferred_element_type=jnp.float32)]
    reduce_scatter x6 -> x0, waiting for transfers between devices: 209 us -> none  [step(): lax.psum_scatter(by_w[name], 'dp', scatter_dimension=0, tiled=True)]
    all_gather x6 -> x0, waiting for transfers between devices: 136 us -> none  [fetched(): lax.all_gather(w[number], 'dp', axis=0, tiled=True)]
    psum x1 -> x0, blocking collectives: 27 us -> none  [step(): squares = lax.psum(sum((jnp.sum(g * g) for g in gradients)), 'dp')]
    unnamed x44 -> x4, local copies, waits for them, and re-layouts: 13.5 us -> 0.01 us
    reduce_sum x4 -> x1, other arithmetic: 7.92 us -> 1.28 us  [step(): factor = jnp.minimum(1.0, 0.5 * lax.rsqrt(jnp.sum(squares) / count + 1e-30))]
  transfers between devices with their start and end apart: 12 -> 0, of which waited for: 10 -> 0; matrix products, arithmetic and copies ran while one was open for 32% -> 0% of each run, Pallas kernels for 0% -> 0%
where the time goes in v1:
time: 229 us
  Pallas kernels  221 us (97%)
  other arithmetic  6.12 us (3%)
    pallas_call x1, Pallas kernels, backward(): pl.pallas_call(functools.partial(backward_kernel, n), out_shape=[jax.Shap...  93.2 us
    pallas_call x1, Pallas kernels, forward(): pl.pallas_call(functools.partial(forward_kernel, n), out_shape=[jax.Shape...  68.8 us
    pallas_call x1, Pallas kernels, top(): pl.pallas_call(top_kernel, grid=(tokens // TILE,), out_shape=[jax.ShapeDt...  59.1 us
    convert_element_type x2, other arithmetic, adamw(): return ((w - 0.02 * step).astype(BF), m, v)  4.84 us

profile of v1, /device:TPU:21, one launch (start us, length us, event | category | flops | bytes accessed | tf_op | source)
XLA Modules:
  0.0 228.5 jit_solution(7863224939611995970)
XLA Ops:
  0.6 68.8 %forward0.1 = (bf16[4096,512]{1,0:T(8,128)(2,1)}, bf16[4096,1280]{1,0:T(8,128)(2,1)}, bf16[4096,512]{1,0:T(8,128)(2,1)}, bf16[4,512,1280]{2,1,0:T(8,128)(2,1)}, ...) custom-call(bf16[4096,512]{1,0:T(8,128)(2,1)} %bitcast.26, bf16[2,32,1280]{2,1,0:T(8,128)(2,1)} %wg_ref.1, ...), custom_call_target="tpu_custom_call" | custom-call | flops 16106127360 | bytes 41943040 | tf_op jit(solution)/shard_map/forward0/pallas_call | solution.py:208
  69.4 59.1 %layer1.1 = (bf16[4096,512]{1,0:T(8,128)(2,1)}, bf16[2,512,1280]{2,1,0:T(8,128)(2,1)}, bf16[1280,512]{1,0:T(8,128)(2,1)}) custom-call(bf16[4096,512]{1,0:T(8,128)(2,1)} %get-tuple-element.23.h1, bf16[4096,512]{1,0:T(8,128)(2,1)} %bitcast.27, bf16[4,512,1280]{2,1,0:T(8,128)(2,1)} %get-tuple-element.24.gu.gu_hbm, bf16[2,1280,512]{2,1,0:T(8,128)(2,1)} %get-tuple-element.25.d), custom_call_target="tpu_custom_call" | custom-call | flops 42949672960 | bytes 25165824 | tf_op jit(solution)/shard_map/layer1/pallas_call | solution.py:275
  128.5 0.0 copy-start
  128.5 0.0 copy-start.1
  128.5 93.2 %backward0.1 = (bf16[2,2,32,1280]{3,2,1,0:T(8,128)(2,1)}, bf16[2,80,512]{2,1,0:T(8,128)(2,1)}, f32[8,128]{1,0:T(8,128)}) custom-call(bf16[4096,512]{1,0:T(8,128)(2,1)} %get-tuple-element.21.a0_hbm, bf16[4096,1280]{1,0:T(8,128)(2,1)} %get-tuple-element.22.hid_hbm, bf16[4096,512]{1,0:T(8,128)(2,1)} %get-tuple-element.26.dh_hbm, ...), custom_call_target="tpu_custom_call" | custom-call | flops 32212254720 | bytes 41943040 | tf_op jit(solution)/shard_map/backward0/pallas_call | solution.py:617
  221.7 1.3 reduce_sum.9
  223.7 0.0 copy-done
  223.7 0.0 copy-done.1
  223.7 2.0 fusion.8
  225.7 2.8 %fusion.2 = (bf16[2,32,1280]{2,1,0:T(8,128)(2,1)}, f32[2,32,1280]{2,1,0:T(8,128)}, f32[2,32,1280]{2,1,0:T(8,128)}, bf16[2,32,1280]{2,1,0:T(8,128)(2,1)}, f32[2,32,1280]{2,1,0:T(8,128)}, /*index=5*/f32[2,32,1280]{2,1,0:T(8,128)}) fusion(bf16[2,32,1280]{2,1,0:T(8,128)(2,1)} %wg_ref.1, f32[]{:T(128)S(6)} %min_shard_map.3, f32[2,32,1280]{2,1,0:T(8,128)} %param.19, ...), kind=kLoop, calls=%fused_computation.11 | loop fusion | flops 2785280 | bytes 3604484 | tf_op jit(solution)/shard_map/convert_element_type | solution.py:667
Async XLA Ops:
  128.5 95.2 %copy-start = (f32[2,80,512]{2,1,0:T(8,128)S(1)}, f32[2,80,512]{2,1,0:T(8,128)}, u32[]{:S(2)}) copy-start(f32[2,80,512]{2,1,0:T(8,128)} %param.21) | copy-start | bytes 983044
  128.5 95.2 %copy-start.1 = (bf16[2,80,512]{2,1,0:T(8,128)(2,1)S(1)}, bf16[2,80,512]{2,1,0:T(8,128)(2,1)}, u32[]{:S(2)}) copy-start(bf16[2,80,512]{2,1,0:T(8,128)(2,1)} %wd_ref.1) | copy-start | bytes 491524

commit v2 on v0

v2 whole, which is shorter than its diff:
```python
import functools

import jax
import jax.numpy as jnp
from jax import lax
from jax.experimental import pallas as pl
from jax.experimental.pallas import tpu as pltpu
from jax.sharding import PartitionSpec as P

MESH = pl.DeviceIdType.MESH
BF, F32 = jnp.bfloat16, jnp.float32
VMEM_LIMIT = 66_500_000
TILE = 512
WIDE = 1024
COLS = 256


def dot(a, b):
    return jnp.dot(a, b, preferred_element_type=F32)


def dot_t(a, b):
    return lax.dot_general(a, b, (((0,), (0,)), ((), ())), preferred_element_type=F32)


def norm_scale(wide):
    return lax.rsqrt(jnp.mean(wide * wide, -1, keepdims=True) + 1e-6)


def places(n):
    nz = n // 2
    me = lax.axis_index("dp")
    z, core = me // 2, me % 2
    return me, z, core, ((z + 1) % nz) * 2 + core, ((z + nz - 1) % nz) * 2 + core, me + 1 - 2 * core


def barrier(devices):
    sem = pltpu.get_barrier_semaphore()
    for device in devices:
        pl.semaphore_signal(sem, inc=1, device_id={"dp": device}, device_id_type=MESH)
    pl.semaphore_wait(sem, len(devices))


def forward_kernel(n, x_hbm, wg_ref, wu_ref, wd_ref, h1_hbm, hid_hbm, a0_hbm, gu_hbm, dt_hbm,
                   x, a0, hid, gu, d, dt, send_sem, recv_sem, in_sem, out_sem):
    nz = n // 2
    me, z, core, right, left, partner = places(n)
    tokens = x.shape[0]
    steps = tokens // TILE
    load = pltpu.make_async_copy(x_hbm, x, in_sem)
    load.start()
    barrier((right, left, partner))

    more, less = nz // 2, nz - 1 - nz // 2
    parts = [
        (wg_ref.at[0], gu, 0, more, less),
        (wu_ref.at[0], gu, 1, less, more),
        (wd_ref.at[0], d, 0, more, less),
        (wg_ref.at[1], gu, 2, less, more),
        (wu_ref.at[1], gu, 3, more, less),
        (wd_ref.at[1], d, 1, less, more),
    ]
    sent = []

    def block(i, chip, which):
        src, whole, first, _, _ = parts[i]
        rows = src.shape[0]
        at = pl.multiple_of((chip * 2 + which) * rows, 16)
        return whole.at[first, pl.ds(at, rows), :]

    def copy(i, k, src, dst, device):
        return pltpu.make_async_remote_copy(
            src_ref=src, dst_ref=dst, send_sem=send_sem.at[i, k], recv_sem=recv_sem.at[i, k],
            device_id={"dp": device}, device_id_type=MESH,
        )

    def send(i, k, src, dst, device):
        c = copy(i, k, src, dst, device)
        c.start()
        sent.append(c)

    def arrived(i, k, at):
        copy(i, k, at, at, partner).wait_recv()

    def begin(i):
        src = parts[i][0]
        own = block(i, z, core)
        send(i, 0, src, own, right)
        send(i, more, src, own, left)
        send(i, 2 * more, src, own, partner)
        rows = src.shape[0]
        whole, first = parts[i][1], parts[i][2]
        whole[first, pl.ds(pl.multiple_of(me * rows, 16), rows), :] = src[...]

    def relay(i, s):
        _, _, _, hops_right, hops_left = parts[i]
        if s <= hops_right:
            at = block(i, (z + nz - s) % nz, core)
            arrived(i, s - 1, at)
            if s < hops_right:
                send(i, s, at, at, right)
            send(i, 2 * more + s, at, at, partner)
        if s <= hops_left:
            at = block(i, (z + s) % nz, core)
            arrived(i, more + s - 1, at)
            if s < hops_left:
                send(i, more + s, at, at, left)
            send(i, 3 * more + s, at, at, partner)

    def finish(i):
        _, _, _, hops_right, hops_left = parts[i]
        arrived(i, 2 * more, block(i, z, 1 - core))
        for s in range(1, hops_right + 1):
            arrived(i, 2 * more + s, block(i, (z + nz - s) % nz, 1 - core))
        for s in range(1, hops_left + 1):
            arrived(i, 3 * more + s, block(i, (z + s) % nz, 1 - core))

    outs = []

    def store(k, src, dst):
        c = pltpu.make_async_copy(src, dst, out_sem.at[k])
        c.start()
        outs.append(c)

    begin(0)
    begin(1)
    load.wait()

    def norm_step(t, _):
        at = pl.ds(pl.multiple_of(t * TILE, TILE), TILE)
        wide = x[at, :].astype(F32)
        a0[at, :] = (wide * norm_scale(wide)).astype(BF)
        return 0

    relay(0, 1)
    relay(1, 1)
    lax.fori_loop(0, steps // 2, norm_step, 0)
    relay(0, 2)
    relay(1, 2)
    lax.fori_loop(steps // 2, steps, norm_step, 0)
    for s in range(3, more + 1):
        relay(0, s)
        relay(1, s)
    begin(2)
    begin(3)
    finish(0)
    finish(1)
    store(0, a0, a0_hbm)

    def up_step(t, _):
        at = pl.ds(pl.multiple_of(t * TILE, TILE), TILE)
        a = a0[at, :]
        gate = dot(a, gu[0])
        up = dot(a, gu[1])
        hid[at, :] = (gate * jax.nn.sigmoid(gate) * up).astype(BF)
        return 0

    def down_step(t, _):
        at = pl.ds(pl.multiple_of(t * TILE, TILE), TILE)
        x[at, :] = x[at, :] + dot(hid[at, :], d[0]).astype(BF)
        return 0

    moves = [(2, 1), (3, 1), (2, 2), (3, 2), (2, 3), (4, 1), (2, 4), (3, 3), (4, 2), (5, 1), (3, 4), (4, 3), (5, 2), (4, 4), (5, 3), (5, 4)]
    starts = {1: 4, 5: 5}
    each = steps // 8
    for q in range(8):
        lax.fori_loop(q * each, (q + 1) * each, up_step, 0)
        relay(*moves[q])
        if q in starts:
            begin(starts[q])
    store(1, hid, hid_hbm)
    store(2, gu.at[pl.ds(0, 2)], gu_hbm.at[pl.ds(0, 2)])
    finish(2)
    for q in range(8):
        lax.fori_loop(q * each, (q + 1) * each, down_step, 0)
        relay(*moves[8 + q])
        if q == 0:
            dt[0] = d[0].T
            store(3, dt.at[0], dt_hbm.at[0])
    store(4, x, h1_hbm)
    finish(3)
    finish(4)
    store(5, gu.at[pl.ds(2, 2)], gu_hbm.at[pl.ds(2, 2)])
    finish(5)
    dt[1] = d[1].T
    store(6, dt.at[1], dt_hbm.at[1])
    for c in sent:
        c.wait_send()
    for c in outs:
        c.wait()


def forward(n, x, wg, wu, wd):
    tokens, dim = x.shape
    hidden = wg.shape[2]
    anyspace, vmem = pl.BlockSpec(memory_space=pl.ANY), pl.BlockSpec(memory_space=pltpu.VMEM)
    shapes = [(tokens, dim), (tokens, hidden), (tokens, dim), (4, dim, hidden), (2, dim, hidden)]
    sems = 4 * (n // 4) + 1
    return pl.pallas_call(
        functools.partial(forward_kernel, n),
        out_shape=[jax.ShapeDtypeStruct(s, BF) for s in shapes],
        in_specs=[anyspace, vmem, vmem, vmem],
        out_specs=[anyspace] * 5,
        scratch_shapes=[
            pltpu.VMEM((tokens, dim), BF),
            pltpu.VMEM((tokens, dim), BF),
            pltpu.VMEM((tokens, hidden), BF),
            pltpu.VMEM((4, dim, hidden), BF),
            pltpu.VMEM((2, hidden, dim), BF),
            pltpu.VMEM((2, dim, hidden), BF),
            pltpu.SemaphoreType.DMA((6, sems)),
            pltpu.SemaphoreType.DMA((6, sems)),
            pltpu.SemaphoreType.DMA,
            pltpu.SemaphoreType.DMA((7,)),
        ],
        compiler_params=pltpu.CompilerParams(collective_id=0, has_side_effects=True, vmem_limit_bytes=VMEM_LIMIT),
        cost_estimate=pl.CostEstimate(flops=6 * tokens * dim * hidden, bytes_accessed=40 << 20, transcendentals=0),
        name="forward0",
    )(x, wg, wu, wd)


def backward_kernel(n, h1_hbm, dy_hbm, a0_hbm, hid_hbm, gu_hbm, dt_hbm, sum_gu, sum_d, factor,
                    h1, a, dh, acc, gu, gt, dt, hid, tgu, td, pgu, pd, rgu, rd, acc_g, acc_u, acc_d, ssq, all_ssq,
                    in_sem, hid_sem, p_send, p_recv, send_gu, recv_gu, send_d, recv_d, q_send, q_recv):
    nz = n // 2
    me, z, core, right, left, partner = places(n)
    tokens, dim = a.shape
    hidden = dt.shape[1]
    nf = hidden // COLS
    last = nz - 1
    rows_g, rows_d = dim // n, hidden // n
    tiles, slots = tokens // TILE, hid.shape[0]
    half = tokens // WIDE // 2

    def load(k, src, dst):
        return pltpu.make_async_copy(src, dst, in_sem.at[k])

    def load_hid(t):
        slot = t % slots
        return pltpu.make_async_copy(hid_hbm.at[pl.ds(pl.multiple_of(t * TILE, TILE), TILE), :], hid.at[slot], hid_sem.at[slot])

    early = [load(0, h1_hbm, h1), load(1, gu_hbm.at[pl.ds(2, 2)], gu), load(2, dy_hbm, dh), load(3, dt_hbm.at[1], dt)]
    later = [load(4, a0_hbm, a), load(5, gu_hbm.at[pl.ds(0, 2)], gu), load(6, dt_hbm.at[0], dt)]
    for c in early:
        c.start()
    for t in range(slots):
        load_hid(t).start()

    sem = pltpu.get_barrier_semaphore()
    for k in range(1, n):
        pl.semaphore_signal(sem, inc=1, device_id={"dp": (me + k) % n}, device_id_type=MESH)
    pl.semaphore_wait(sem, n - 1)

    ssq[...] = jnp.zeros_like(ssq)
    early[0].wait()

    def begin_step(t, _):
        at = pl.ds(pl.multiple_of(t * TILE, TILE), TILE)
        wide = h1[at, :].astype(F32)
        a[at, :] = (wide * norm_scale(wide)).astype(BF)
        acc[at, :] = jnp.zeros((TILE, dim), F32)
        return 0

    lax.fori_loop(0, tiles, begin_step, 0)
    early[1].wait()
    gt[0] = gu[0].T
    gt[1] = gu[1].T
    early[2].wait()
    early[3].wait()

    def over_gu(q):
        return pltpu.make_async_remote_copy(
            src_ref=tgu.at[q, :, :, 1 - core], dst_ref=pgu.at[q], send_sem=p_send.at[q], recv_sem=p_recv.at[q],
            device_id={"dp": partner}, device_id_type=MESH,
        )

    def over_d(layer):
        k = 2 * nf + layer
        return pltpu.make_async_remote_copy(
            src_ref=td.at[layer, :, 1 - core], dst_ref=pd.at[layer], send_sem=p_send.at[k], recv_sem=p_recv.at[k],
            device_id={"dp": partner}, device_id_type=MESH,
        )

    def chip(way, s):
        return (z + 2 * nz - 1 - s) % nz if way == 0 else (z + 1 + s) % nz

    def squared(v):
        g = v.astype(F32)
        g = g * g
        while g.ndim > 2:
            g = jnp.sum(g, axis=0)
        g = jnp.sum(g, axis=0, keepdims=True)
        total = g[:, 0:128]
        for k in range(1, g.shape[1] // 128):
            total = total + g[:, k * 128 : (k + 1) * 128]
        ssq[0:1, :] += total

    class Gu:
        def __init__(self, q):
            self.q = q

        def cols(self, way):
            return slice(way * (COLS // 2), (way + 1) * (COLS // 2))

        def term(self, way, b):
            return tgu[self.q, :, b, core, :, self.cols(way)].astype(F32) + pgu[self.q, :, b, :, self.cols(way)].astype(F32)

        def keep(self, way, b, v):
            tgu[self.q, :, b, core, :, self.cols(way)] = v

        def got(self, way, s):
            return rgu[self.q, way, s].astype(F32)

        def move(self, way, s):
            return pltpu.make_async_remote_copy(
                src_ref=tgu.at[self.q, :, chip(way, s), core, :, pl.ds(way * (COLS // 2), COLS // 2)], dst_ref=rgu.at[self.q, way, s],
                send_sem=send_gu.at[self.q, way, s], recv_sem=recv_gu.at[self.q, way, s],
                device_id={"dp": right if way == 0 else left}, device_id_type=MESH,
            )

        def put(self, way, v):
            layer, j = 1 - self.q // nf, self.q % nf
            w = COLS // 2
            sum_gu[layer, :, :, pl.ds(pl.multiple_of(j * COLS + way * w, w), w)] = v

    class Down:
        def __init__(self, layer):
            self.layer = layer

        def cols(self, way):
            return slice(way * (dim // 2), (way + 1) * (dim // 2))

        def term(self, way, b):
            return td[self.layer, b, core, :, self.cols(way)].astype(F32) + pd[self.layer, b, :, self.cols(way)].astype(F32)

        def keep(self, way, b, v):
            td[self.layer, b, core, :, self.cols(way)] = v

        def got(self, way, s):
            return rd[self.layer, way, s].astype(F32)

        def move(self, way, s):
            return pltpu.make_async_remote_copy(
                src_ref=td.at[self.layer, chip(way, s), core, :, pl.ds(way * (dim // 2), dim // 2)], dst_ref=rd.at[self.layer, way, s],
                send_sem=send_d.at[self.layer, way, s], recv_sem=recv_d.at[self.layer, way, s],
                device_id={"dp": right if way == 0 else left}, device_id_type=MESH,
            )

        def put(self, way, v):
            sum_d[self.layer, :, self.cols(way)] = v

    def event(part, s):
        @pl.when(s == 0)
        def _():
            for way in range(2):
                part.keep(way, chip(way, s), part.term(way, chip(way, s)).astype(BF))
            for way in range(2):
                part.move(way, s).start()

        @pl.when(jnp.logical_and(s > 0, s < last))
        def _():
            for way in range(2):
                part.move(way, s - 1).wait_recv()
                part.keep(way, chip(way, s), (part.got(way, s - 1) + part.term(way, chip(way, s))).astype(BF))
                part.move(way, s).start()

        @pl.when(s == last)
        def _():
            for way in range(2):
                part.move(way, s - 1).wait_recv()
                v = (part.got(way, s - 1) + part.term(way, chip(way, s))).astype(BF)
                part.put(way, v)
                squared(v)

    first_top, first_down, first_low = 0, 2 * nf, 2 * nf + 2
    end_low = first_low + 2 * nf

    def ready(q):
        return 2 * (q + q // nf)

    def events(p):
        def each_gu(q, _):
            s = p - (ready(q) + 2)

            @pl.when(jnp.logical_and(s >= 0, s <= last))
            def _():
                @pl.when(s == 0)
                def _():
                    over_gu(q).wait_recv()

                event(Gu(q), s)

            return 0

        def each_d(k, _):
            layer = 1 - k
            s = p - (first_down + 2 * k)

            @pl.when(jnp.logical_and(s >= 0, s <= last))
            def _():
                @pl.when(s == 0)
                def _():
                    over_d(layer).wait_recv()

                event(Down(layer), s)

            return 0

        lax.fori_loop(0, 2, each_d, 0)
        lax.fori_loop(0, 2 * nf, each_gu, 0)

    def grads(q):
        for b in range(nz):
            for c in range(2):
                k = (b * 2 + c) * rows_g
                tgu[q, 0, b, c] = acc_g[k : k + rows_g, :].astype(BF)
                tgu[q, 1, b, c] = acc_u[k : k + rows_g, :].astype(BF)
        over_gu(q).start()

    def wide_step(j, with_top):
        cols = pl.ds(pl.multiple_of(j * COLS, COLS), COLS)

        def body(t, _):
            at = pl.ds(pl.multiple_of(t * WIDE, WIDE), WIDE)
            rows = a[at, :]
            by_y = dh[at, :]
            gate = dot(rows, gu[0, :, cols])
            up = dot(rows, gu[1, :, cols])
            by_hid = dot(by_y, dt[:, cols]).astype(BF).astype(F32)
            sig = jax.nn.sigmoid(gate)
            act = gate * sig
            by_up = (by_hid * act).astype(BF)
            by_gate = (by_hid * up * (sig + act * (1.0 - sig))).astype(BF)
            acc_g[...] += dot_t(rows, by_gate)
            acc_u[...] += dot_t(rows, by_up)
            if with_top:
                acc_d[...] += dot_t(by_y, (act * up).astype(BF))
                acc[at, :] += dot(by_gate, gt[0, cols, :]) + dot(by_up, gt[1, cols, :])
            return 0

        return body

    def top_end(t, _):
        at = pl.ds(pl.multiple_of(t * TILE, TILE), TILE)
        wide = h1[at, :].astype(F32)
        scale = norm_scale(wide)
        by_a = acc[at, :].astype(BF).astype(F32)
        by_h = scale * by_a - wide * (scale * scale * scale * jnp.mean(by_a * wide, -1, keepdims=True))
        dh[at, :] = dh[at, :] + by_h.astype(BF)
        return 0

    def down_step(t, _):
        load_hid(t).wait()
        acc[0:hidden, :] += dot_t(hid[t % slots], dh[pl.ds(pl.multiple_of(t * TILE, TILE), TILE), :])

        @pl.when(t + slots < tiles)
        def _():
            load_hid(t + slots).start()

        return 0

    def zero():
        acc_g[...] = jnp.zeros_like(acc_g)
        acc_u[...] = jnp.zeros_like(acc_u)

    def phase(p, _):
        part_of = p % 2
        lo = part_of * half

        @pl.when(p < first_down)
        def _():
            j = p // 2

            @pl.when(part_of == 0)
            def _():
                zero()
                acc_d[...] = jnp.zeros_like(acc_d)

            lax.fori_loop(lo, lo + half, wide_step(j, True), 0)

            @pl.when(part_of == 1)
            def _():
                grads(j)
                down = acc_d[...].T.astype(BF)
                for i in range(COLS // 16):
                    row = j * COLS + i * 16
                    device = row // rows_d
                    td[1, device // 2, device % 2, pl.ds(pl.multiple_of(row % rows_d, 16), 16), :] = down[i * 16 : i * 16 + 16, :]

            @pl.when(p == first_down - 1)
            def _():
                over_d(1).start()
                for c in later:
                    c.start()
                lax.fori_loop(0, tiles, top_end, 0)

        @pl.when(jnp.logical_and(p >= first_down, p < first_low))
        def _():
            @pl.when(part_of == 0)
            def _():
                acc[0:hidden, :] = jnp.zeros((hidden, dim), F32)

            lax.fori_loop(part_of * (tiles // 2), part_of * (tiles // 2) + tiles // 2, down_step, 0)

            @pl.when(part_of == 1)
            def _():
                for b in range(nz):
                    for c in range(2):
                        k = (b * 2 + c) * rows_d
                        td[0, b, c] = acc[k : k + rows_d, :].astype(BF)
                over_d(0).start()
                for c in later:
                    c.wait()

        @pl.when(jnp.logical_and(p >= first_low, p < end_low))
        def _():
            j = (p - first_low) // 2

            @pl.when(part_of == 0)
            def _():
                zero()

            lax.fori_loop(lo, lo + half, wide_step(j, False), 0)

            @pl.when(part_of == 1)
            def _():
                grads(nf + j)

        events(p)
        return 0

    lax.fori_loop(0, end_low + nz, phase, 0)

    all_ssq[me] = ssq[...]

    def scalar(k, slot):
        return pltpu.make_async_remote_copy(
            src_ref=ssq, dst_ref=all_ssq.at[slot], send_sem=q_send.at[k], recv_sem=q_recv.at[k],
            device_id={"dp": (me + k) % n}, device_id_type=MESH,
        )

    def tell(k, _):
        scalar(k, me).start()
        return 0

    lax.fori_loop(1, n, tell, 0)

    def left_gu(q, _):
        over_gu(q).wait_send()

        def one(s, _):
            for way in range(2):
                Gu(q).move(way, s).wait_send()
            return 0

        lax.fori_loop(0, last, one, 0)
        return 0

    def left_d(layer, _):
        over_d(layer).wait_send()

        def one(s, _):
            for way in range(2):
                Down(layer).move(way, s).wait_send()
            return 0

        lax.fori_loop(0, last, one, 0)
        return 0

    lax.fori_loop(0, 2 * nf, left_gu, 0)
    lax.fori_loop(0, 2, left_d, 0)

    def told(k, _):
        scalar(k, (me + n - k) % n).wait()
        return 0

    lax.fori_loop(1, n, told, 0)
    total = jnp.sum(jnp.sum(jnp.sum(all_ssq[...], axis=0), axis=0, keepdims=True), axis=1, keepdims=True)
    count = 3 * 2 * dim * hidden
    factor[...] = jnp.broadcast_to(jnp.minimum(1.0, 0.5 * lax.rsqrt(total / count + 1e-30)), factor.shape)


def backward(n, h1, dy, a0, hid, gu, dt):
    nz = n // 2
    tokens, dim = a0.shape
    hidden = dt.shape[2]
    nf, last = hidden // COLS, nz - 1
    rg, rd = dim // n, hidden // n
    anyspace, vmem = pl.BlockSpec(memory_space=pl.ANY), pl.BlockSpec(memory_space=pltpu.VMEM)
    V = lambda *s: pltpu.VMEM(s, BF)
    W = lambda *s: pltpu.VMEM(s, F32)
    S = lambda *s: pltpu.SemaphoreType.DMA(s)
    return pl.pallas_call(
        functools.partial(backward_kernel, n),
        out_shape=[
            jax.ShapeDtypeStruct((2, 2, rg, hidden), BF),
            jax.ShapeDtypeStruct((2, rd, dim), BF),
            jax.ShapeDtypeStruct((8, 128), F32),
        ],
        in_specs=[anyspace] * 6,
        out_specs=[vmem] * 3,
        scratch_shapes=[
            V(tokens, dim),
            V(tokens, dim),
            V(tokens, dim),
            W(tokens, dim),
            V(2, dim, hidden),
            V(2, hidden, dim),
            V(dim, hidden),
            V(3, TILE, hidden),
            V(2 * nf, 2, nz, 2, rg, COLS),
            V(2, nz, 2, rd, dim),
            V(2 * nf, 2, nz, rg, COLS),
            V(2, nz, rd, dim),
            V(2 * nf, 2, last, 2, rg, COLS // 2),
            V(2, 2, last, rd, dim // 2),
            W(dim, COLS),
            W(dim, COLS),
            W(dim, COLS),
            W(8, 128),
            W(n, 8, 128),
            S(7),
            S(3),
            S(2 * nf + 2),
            S(2 * nf + 2),
            S(2 * nf, 2, last),
            S(2 * nf, 2, last),
            S(2, 2, last),
            S(2, 2, last),
            S(n),
            S(n),
        ],
        compiler_params=pltpu.CompilerParams(collective_id=1, has_side_effects=True, vmem_limit_bytes=VMEM_LIMIT),
        cost_estimate=pl.CostEstimate(flops=28 * tokens * dim * hidden, bytes_accessed=40 << 20, transcendentals=0),
        name="backward",
    )(h1, dy, a0, hid, gu, dt)


def adamw(w, m, v, g):
    m = 0.9 * m + 0.1 * g
    v = 0.95 * v + 0.05 * g * g
    step = m * lax.rsqrt(v + 1e-8) + 0.1 * w
    return (w - 0.02 * step).astype(BF), m, v


def solution(mesh):
    n = mesh.shape["dp"]

    def step(x, dy, *arrays):
        weights, m, v = (arrays[i : i + 3] for i in (0, 3, 6))
        h1, hid, a0, gu, dt = forward(n, x[0], *weights)
        sum_gu, sum_d, factor = backward(n, h1, dy[0], a0, hid, gu, dt)
        gradients = [sum_gu[:, 0].astype(F32), sum_gu[:, 1].astype(F32), sum_d.astype(F32)]
        factor = factor[0, 0]
        new = [adamw(w.astype(F32), m, v, g * factor) for w, m, v, g in zip(weights, m, v, gradients, strict=True)]
        return tuple(one[which] for which in range(3) for one in new)

    states, cut = P(("rep", "dp"), None, None), P(None, "dp", None)
    return jax.shard_map(
        step,
        mesh=mesh,
        in_specs=(states, states) + (cut,) * 9,
        out_specs=(P("rep", "dp", None),) * 9,
        check_vma=False,
    )
```

time: 656 us -> 234 us (0.36); the launches traced: 646 us -> 234 us
  waiting for transfers between devices: 347 us -> 0 us
  Pallas kernels: 0 us -> 226 us
  matrix products: 220 us -> 0 us
  blocking collectives: 27 us -> 0 us
  local copies, waits for them, and re-layouts: 18.3 us -> 1.2 us
  between operations: 17.6 us -> 0.68 us
  other arithmetic: 15 us -> 5.96 us
    pallas_call x0 -> x2, Pallas kernels: none -> 226 us  [the longest x1 160 us: backward(): pl.pallas_call(functools.partial(backward_kernel, n), out_shape=[jax.Shap...]
    dot_general x15 -> x0, matrix products: 220 us -> none  [the longest x5 82.1 us: layer(): gate = jnp.dot(a, w['w_gate'], preferred_element_type=jnp.float32)]
    reduce_scatter x6 -> x0, waiting for transfers between devices: 209 us -> none  [step(): lax.psum_scatter(by_w[name], 'dp', scatter_dimension=0, tiled=True)]
    all_gather x6 -> x0, waiting for transfers between devices: 136 us -> none  [fetched(): lax.all_gather(w[number], 'dp', axis=0, tiled=True)]
    psum x1 -> x0, blocking collectives: 27 us -> none  [step(): squares = lax.psum(sum((jnp.sum(g * g) for g in gradients)), 'dp')]
    unnamed x44 -> x4, local copies, waits for them, and re-layouts: 13.5 us -> 0.01 us
    reduce_sum x4 -> x0, other arithmetic: 7.92 us -> none  [the longest x3 4.85 us: step(): squares = lax.psum(sum((jnp.sum(g * g) for g in gradients)), 'dp')]
  transfers between devices with their start and end apart: 12 -> 0, of which waited for: 10 -> 0; matrix products, arithmetic and copies ran while one was open for 32% -> 0% of each run, Pallas kernels for 0% -> 0%
where the time goes in v2:
time: 234 us
  Pallas kernels  226 us (97%)
  other arithmetic  5.96 us (3%)
    pallas_call x1, Pallas kernels, backward(): pl.pallas_call(functools.partial(backward_kernel, n), out_shape=[jax.Shap...  160 us
    pallas_call x1, Pallas kernels, forward(): pl.pallas_call(functools.partial(forward_kernel, n), out_shape=[jax.Shape...  66.4 us
    convert_element_type x2, other arithmetic, adamw(): return ((w - 0.02 * step).astype(BF), m, v)  5.96 us

profile of v2, /device:TPU:21, one launch (start us, length us, event | category | flops | bytes accessed | tf_op | source)
XLA Modules:
  0.0 234.3 jit_solution(32175039860785292)
XLA Ops:
  0.6 66.4 %forward0.1 = (bf16[4096,512]{1,0:T(8,128)(2,1)}, bf16[4096,1280]{1,0:T(8,128)(2,1)}, bf16[4096,512]{1,0:T(8,128)(2,1)}, bf16[4,512,1280]{2,1,0:T(8,128)(2,1)}, bf16[2,512,1280]{2,1,0:T(8,128)(2,1)}) custom-call(bf16[4096,512]{1,0:T(8,128)(2,1)} %bitcast.25, bf16[2,32,1280]{2,1,0:T(8,128)(2,1)} %wg_ref.1, bf16[2,32,1280]{2,1,0:T(8,128)(2,1)} %wu_ref.1, ...), custom_call_target="tpu_custom_call" | custom-call | flops 16106127360 | bytes 41943040 | tf_op jit(solution)/shard_map/forward0/pallas_call | solution.py:199
  67.1 0.0 copy-start
  67.1 0.0 copy-start.1
  67.1 160.0 %backward.1 = (bf16[2,2,32,1280]{3,2,1,0:T(8,128)(2,1)}, bf16[2,80,512]{2,1,0:T(8,128)(2,1)}, f32[8,128]{1,0:T(8,128)}) custom-call(bf16[4096,512]{1,0:T(8,128)(2,1)} %get-tuple-element.17.h1_hbm, bf16[4096,512]{1,0:T(8,128)(2,1)} %bitcast.26, bf16[4096,512]{1,0:T(8,128)(2,1)} %get-tuple-element.18.a0_hbm, bf16[4096,1280]{1,0:T(8,128)(2,1)} %get-tuple-element.19.hid_hbm, ...), custom_call_target="tpu_custom_call" | custom-call | flops 75161927680 | bytes 41943040 | tf_op jit(solution)/shard_map/backward/pallas_call | solution.py:593
  227.1 1.2 slice.10
  228.3 0.0 copy-done
  228.3 0.0 copy-done.1
  228.3 2.6 %fusion.8 = (bf16[2,80,512]{2,1,0:T(8,128)(2,1)}, f32[2,80,512]{2,1,0:T(8,128)}, f32[2,80,512]{2,1,0:T(8,128)}) fusion(bf16[2,80,512]{2,1,0:T(8,128)(2,1)S(1)} %copy-done.1, f32[]{:T(128)} %bitcast.2, bf16[2,80,512]{2,1,0:T(8,128)(2,1)} %get-tuple-element.24, f32[2,80,512]{2,1,0:T(8,128)S(1)} %copy-done, f32[2,80,512]{2,1,0:T(8,128)} %param.18), kind=kLoop, calls=%fused_computation.17 | loop fusion | flops 1392640 | bytes 1802244 | tf_op jit(solution)/shard_map/convert_element_type | solution.py:643
  230.9 3.4 %fusion.2 = (bf16[2,32,1280]{2,1,0:T(8,128)(2,1)}, f32[2,32,1280]{2,1,0:T(8,128)}, f32[2,32,1280]{2,1,0:T(8,128)}, bf16[2,32,1280]{2,1,0:T(8,128)(2,1)}, f32[2,32,1280]{2,1,0:T(8,128)}, /*index=5*/f32[2,32,1280]{2,1,0:T(8,128)}) fusion(bf16[2,32,1280]{2,1,0:T(8,128)(2,1)} %wg_ref.1, f32[]{:T(128)} %bitcast.2, f32[2,32,1280]{2,1,0:T(8,128)} %param.19, ...), kind=kLoop, calls=%fused_computation.11 | loop fusion | flops 2785280 | bytes 3604484 | tf_op jit(solution)/shard_map/convert_element_type | solution.py:643
Async XLA Ops:
  67.1 161.2 %copy-start = (f32[2,80,512]{2,1,0:T(8,128)S(1)}, f32[2,80,512]{2,1,0:T(8,128)}, u32[]{:S(2)}) copy-start(f32[2,80,512]{2,1,0:T(8,128)} %param.21) | copy-start | bytes 983044
  67.1 161.2 %copy-start.1 = (bf16[2,80,512]{2,1,0:T(8,128)(2,1)S(1)}, bf16[2,80,512]{2,1,0:T(8,128)(2,1)}, u32[]{:S(2)}) copy-start(bf16[2,80,512]{2,1,0:T(8,128)(2,1)} %wd_ref.1) | copy-start | bytes 491524

commit v3 on v2

--- a/solution.py
+++ b/solution.py
@@ -13,6 +13,8 @@
 TILE = 512
 WIDE = 1024
 COLS = 256
+DIRECT = 3
+WAIT = 4
 
 
 def dot(a, b):
@@ -41,7 +43,7 @@
     pl.semaphore_wait(sem, len(devices))
 
 
-def forward_kernel(n, x_hbm, wg_ref, wu_ref, wd_ref, h1_hbm, hid_hbm, a0_hbm, gu_hbm, dt_hbm,
+def forward_kernel(n, x_hbm, wg_ref, wu_ref, wd_ref, h1_hbm, a1_hbm, hid_hbm, a0_hbm, gu_hbm, dt_hbm,
                    x, a0, hid, gu, d, dt, send_sem, recv_sem, in_sem, out_sem):
     nz = n // 2
     me, z, core, right, left, partner = places(n)
@@ -52,21 +54,24 @@
     barrier((right, left, partner))
 
     more, less = nz // 2, nz - 1 - nz // 2
-    parts = [
-        (wg_ref.at[0], gu, 0, more, less),
-        (wu_ref.at[0], gu, 1, less, more),
-        (wd_ref.at[0], d, 0, more, less),
-        (wg_ref.at[1], gu, 2, less, more),
-        (wu_ref.at[1], gu, 3, more, less),
-        (wd_ref.at[1], d, 1, less, more),
+    g_rows, d_rows = wg_ref.shape[1], wd_ref.shape[1]
+    g_half = g_rows // 2
+    parts = []
+    for lo in (0, g_half):
+        parts.append((wg_ref.at[0, pl.ds(lo, g_half)], g_rows, lo, gu, 0, more, less))
+        parts.append((wu_ref.at[0, pl.ds(lo, g_half)], g_rows, lo, gu, 1, less, more))
+    parts += [
+        (wd_ref.at[0], d_rows, 0, d, 0, more, less),
+        (wg_ref.at[1], g_rows, 0, gu, 2, less, more),
+        (wu_ref.at[1], g_rows, 0, gu, 3, more, less),
+        (wd_ref.at[1], d_rows, 0, d, 1, less, more),
     ]
     sent = []
 
     def block(i, chip, which):
-        src, whole, first, _, _ = parts[i]
-        rows = src.shape[0]
-        at = pl.multiple_of((chip * 2 + which) * rows, 16)
-        return whole.at[first, pl.ds(at, rows), :]
+        src, rows, lo, whole, first, _, _ = parts[i]
+        at = pl.multiple_of((chip * 2 + which) * rows + lo, 16)
+        return whole.at[first, pl.ds(at, src.shape[0]), :]
 
     def copy(i, k, src, dst, device):
         return pltpu.make_async_remote_copy(
@@ -83,17 +88,15 @@
         copy(i, k, at, at, partner).wait_recv()
 
     def begin(i):
-        src = parts[i][0]
+        src, rows, lo, whole, first, _, _ = parts[i]
         own = block(i, z, core)
         send(i, 0, src, own, right)
         send(i, more, src, own, left)
         send(i, 2 * more, src, own, partner)
-        rows = src.shape[0]
-        whole, first = parts[i][1], parts[i][2]
-        whole[first, pl.ds(pl.multiple_of(me * rows, 16), rows), :] = src[...]
+        whole[first, pl.ds(pl.multiple_of(me * rows + lo, 16), src.shape[0]), :] = src[...]
 
     def relay(i, s):
-        _, _, _, hops_right, hops_left = parts[i]
+        hops_right, hops_left = parts[i][5:]
         if s <= hops_right:
             at = block(i, (z + nz - s) % nz, core)
             arrived(i, s - 1, at)
@@ -108,7 +111,7 @@
             send(i, 3 * more + s, at, at, partner)
 
     def finish(i):
-        _, _, _, hops_right, hops_left = parts[i]
+        hops_right, hops_left = parts[i][5:]
         arrived(i, 2 * more, block(i, z, 1 - core))
         for s in range(1, hops_right + 1):
             arrived(i, 2 * more + s, block(i, (z + nz - s) % nz, 1 - core))
@@ -122,8 +125,8 @@
         c.start()
         outs.append(c)
 
-    begin(0)
-    begin(1)
+    for i in range(4):
+        begin(i)
     load.wait()
 
     def norm_step(t, _):
@@ -132,19 +135,17 @@
         a0[at, :] = (wide * norm_scale(wide)).astype(BF)
         return 0
 
-    relay(0, 1)
-    relay(1, 1)
-    lax.fori_loop(0, steps // 2, norm_step, 0)
-    relay(0, 2)
-    relay(1, 2)
-    lax.fori_loop(steps // 2, steps, norm_step, 0)
-    for s in range(3, more + 1):
-        relay(0, s)
-        relay(1, s)
-    begin(2)
-    begin(3)
-    finish(0)
-    finish(1)
+    for s in range(1, more):
+        if s < 3:
+            lax.fori_loop((s - 1) * (steps // 2), s * (steps // 2), norm_step, 0)
+        for i in range(4):
+            relay(i, s)
+    for i in range(4, 7):
+        begin(i)
+    for i in range(4):
+        relay(i, more)
+    for i in range(4):
+        finish(i)
     store(0, a0, a0_hbm)
 
     def up_step(t, _):
@@ -157,36 +158,45 @@
 
     def down_step(t, _):
         at = pl.ds(pl.multiple_of(t * TILE, TILE), TILE)
-        x[at, :] = x[at, :] + dot(hid[at, :], d[0]).astype(BF)
-        return 0
-
-    moves = [(2, 1), (3, 1), (2, 2), (3, 2), (2, 3), (4, 1), (2, 4), (3, 3), (4, 2), (5, 1), (3, 4), (4, 3), (5, 2), (4, 4), (5, 3), (5, 4)]
-    starts = {1: 4, 5: 5}
+        h = x[at, :] + dot(hid[at, :], d[0]).astype(BF)
+        x[at, :] = h
+        wide = h.astype(F32)
+        a0[at, :] = (wide * norm_scale(wide)).astype(BF)
+        return 0
+
+    moves = [
+        [(4, 1)], [(5, 1)], [(4, 2), (6, 1)], [(5, 2)], [(4, 3)], [(6, 2)], [(4, 4)], [(5, 3), (7, 1)],
+        [(6, 3)], [], [(5, 4)], [(7, 2)], [], [(6, 4)], [(7, 3)], [(7, 4)],
+    ]
     each = steps // 8
     for q in range(8):
         lax.fori_loop(q * each, (q + 1) * each, up_step, 0)
-        relay(*moves[q])
-        if q in starts:
-            begin(starts[q])
+        for k in moves[q]:
+            relay(*k)
+        if q == 3:
+            begin(7)
     store(1, hid, hid_hbm)
     store(2, gu.at[pl.ds(0, 2)], gu_hbm.at[pl.ds(0, 2)])
-    finish(2)
+    outs[0].wait()
+    finish(4)
     for q in range(8):
         lax.fori_loop(q * each, (q + 1) * each, down_step, 0)
-        relay(*moves[8 + q])
+        for k in moves[8 + q]:
+            relay(*k)
         if q == 0:
             dt[0] = d[0].T
             store(3, dt.at[0], dt_hbm.at[0])
     store(4, x, h1_hbm)
-    finish(3)
-    finish(4)
+    store(7, a0, a1_hbm)
+    finish(5)
+    finish(6)
     store(5, gu.at[pl.ds(2, 2)], gu_hbm.at[pl.ds(2, 2)])
-    finish(5)
+    finish(7)
     dt[1] = d[1].T
     store(6, dt.at[1], dt_hbm.at[1])
     for c in sent:
         c.wait_send()
-    for c in outs:
+    for c in outs[1:]:
         c.wait()
 
 
@@ -194,13 +204,13 @@
     tokens, dim = x.shape
     hidden = wg.shape[2]
     anyspace, vmem = pl.BlockSpec(memory_space=pl.ANY), pl.BlockSpec(memory_space=pltpu.VMEM)
-    shapes = [(tokens, dim), (tokens, hidden), (tokens, dim), (4, dim, hidden), (2, dim, hidden)]
+    shapes = [(tokens, dim), (tokens, dim), (tokens, hidden), (tokens, dim), (4, dim, hidden), (2, dim, hidden)]
     sems = 4 * (n // 4) + 1
     return pl.pallas_call(
         functools.partial(forward_kernel, n),
         out_shape=[jax.ShapeDtypeStruct(s, BF) for s in shapes],
         in_specs=[anyspace, vmem, vmem, vmem],
-        out_specs=[anyspace] * 5,
+        out_specs=[anyspace] * 6,
         scratch_shapes=[
             pltpu.VMEM((tokens, dim), BF),
             pltpu.VMEM((tokens, dim), BF),
@@ -208,10 +218,10 @@
             pltpu.VMEM((4, dim, hidden), BF),
             pltpu.VMEM((2, hidden, dim), BF),
             pltpu.VMEM((2, dim, hidden), BF),
-            pltpu.SemaphoreType.DMA((6, sems)),
-            pltpu.SemaphoreType.DMA((6, sems)),
+            pltpu.SemaphoreType.DMA((8, sems)),
+            pltpu.SemaphoreType.DMA((8, sems)),
             pltpu.SemaphoreType.DMA,
-            pltpu.SemaphoreType.DMA((7,)),
+            pltpu.SemaphoreType.DMA((8,)),
         ],
         compiler_params=pltpu.CompilerParams(collective_id=0, has_side_effects=True, vmem_limit_bytes=VMEM_LIMIT),
         cost_estimate=pl.CostEstimate(flops=6 * tokens * dim * hidden, bytes_accessed=40 << 20, transcendentals=0),
@@ -219,9 +229,9 @@
     )(x, wg, wu, wd)
 
 
-def backward_kernel(n, h1_hbm, dy_hbm, a0_hbm, hid_hbm, gu_hbm, dt_hbm, sum_gu, sum_d, factor,
-                    h1, a, dh, acc, gu, gt, dt, hid, tgu, td, pgu, pd, rgu, rd, acc_g, acc_u, acc_d, ssq, all_ssq,
-                    in_sem, hid_sem, p_send, p_recv, send_gu, recv_gu, send_d, recv_d, q_send, q_recv):
+def backward_kernel(n, h1_hbm, a1_hbm, dy_hbm, a0_hbm, hid_hbm, gu_hbm, dt_hbm, sum_gu, sum_d, factor,
+                    h1, a, dh, acc, gu, gt, dt, hid, tgu, td, pgu, pd, rgu, rd, rs, acc_gu, acc_d, ssq, all_ssq,
+                    in_sem, hid_sem, p_send, p_recv, send_gu, recv_gu, send_d, recv_d, send_s, recv_s, q_send, q_recv):
     nz = n // 2
     me, z, core, right, left, partner = places(n)
     tokens, dim = a.shape
@@ -239,7 +249,7 @@
         slot = t % slots
         return pltpu.make_async_copy(hid_hbm.at[pl.ds(pl.multiple_of(t * TILE, TILE), TILE), :], hid.at[slot], hid_sem.at[slot])
 
-    early = [load(0, h1_hbm, h1), load(1, gu_hbm.at[pl.ds(2, 2)], gu), load(2, dy_hbm, dh), load(3, dt_hbm.at[1], dt)]
+    early = [load(1, gu_hbm.at[pl.ds(2, 2)], gu), load(7, a1_hbm, a), load(2, dy_hbm, dh), load(3, dt_hbm.at[1], dt), load(0, h1_hbm, h1)]
     later = [load(4, a0_hbm, a), load(5, gu_hbm.at[pl.ds(0, 2)], gu), load(6, dt_hbm.at[0], dt)]
     for c in early:
         c.start()
@@ -252,21 +262,18 @@
     pl.semaphore_wait(sem, n - 1)
 
     ssq[...] = jnp.zeros_like(ssq)
+
+    def begin_step(t, _):
+        acc[pl.ds(pl.multiple_of(t * TILE, TILE), TILE), :] = jnp.zeros((TILE, dim), F32)
+        return 0
+
+    lax.fori_loop(0, tiles, begin_step, 0)
     early[0].wait()
-
-    def begin_step(t, _):
-        at = pl.ds(pl.multiple_of(t * TILE, TILE), TILE)
-        wide = h1[at, :].astype(F32)
-        a[at, :] = (wide * norm_scale(wide)).astype(BF)
-        acc[at, :] = jnp.zeros((TILE, dim), F32)
-        return 0
-
-    lax.fori_loop(0, tiles, begin_step, 0)
-    early[1].wait()
-    gt[0] = gu[0].T
-    gt[1] = gu[1].T
-    early[2].wait()
-    early[3].wait()
+    for j in range(nf):
+        for i in range(2):
+            gt[j, i * COLS : (i + 1) * COLS, :] = gu[i, :, j * COLS : (j + 1) * COLS].T
+    for c in early[1:4]:
+        c.wait()
 
     def over_gu(q):
         return pltpu.make_async_remote_copy(
@@ -299,6 +306,9 @@
         def __init__(self, q):
             self.q = q
 
+        def over(self):
+            return over_gu(self.q)
+
         def cols(self, way):
             return slice(way * (COLS // 2), (way + 1) * (COLS // 2))
 
@@ -327,6 +337,9 @@
         def __init__(self, layer):
             self.layer = layer
 
+        def over(self):
+            return over_d(self.layer)
+
         def cols(self, way):
             return slice(way * (dim // 2), (way + 1) * (dim // 2))
 
@@ -352,6 +365,7 @@
     def event(part, s):
         @pl.when(s == 0)
         def _():
+            part.over().wait()
             for way in range(2):
                 part.keep(way, chip(way, s), part.term(way, chip(way, s)).astype(BF))
             for way in range(2):
@@ -360,14 +374,14 @@
         @pl.when(jnp.logical_and(s > 0, s < last))
         def _():
             for way in range(2):
-                part.move(way, s - 1).wait_recv()
+                part.move(way, s - 1).wait()
                 part.keep(way, chip(way, s), (part.got(way, s - 1) + part.term(way, chip(way, s))).astype(BF))
                 part.move(way, s).start()
 
         @pl.when(s == last)
         def _():
             for way in range(2):
-                part.move(way, s - 1).wait_recv()
+                part.move(way, s - 1).wait()
                 v = (part.got(way, s - 1) + part.term(way, chip(way, s))).astype(BF)
                 part.put(way, v)
                 squared(v)
@@ -378,43 +392,78 @@
     def ready(q):
         return 2 * (q + q // nf)
 
+    rings = 2 * nf - DIRECT
+    order = sorted(range(1, nz), key=lambda k: -min(k, nz - k))
+
+    def straight(i, k):
+        to = (z + k) % nz
+        return pltpu.make_async_remote_copy(
+            src_ref=tgu.at[rings + i, :, to, core], dst_ref=rs.at[i, k], send_sem=send_s.at[i, k], recv_sem=recv_s.at[i, k],
+            device_id={"dp": to * 2 + core}, device_id_type=MESH,
+        )
+
+    def both_terms(q, b):
+        return tgu[q, :, b, core].astype(F32) + pgu[q, :, b].astype(F32)
+
     def events(p):
+        def each_direct(i, _):
+            q = rings + i
+            s = p - (ready(q) + 2)
+
+            @pl.when(s == 0)
+            def _():
+                over_gu(q).wait()
+                for k in order:
+                    to = (z + k) % nz
+                    tgu[q, :, to, core] = both_terms(q, to).astype(BF)
+                    straight(i, k).start()
+
+            @pl.when(s == WAIT)
+            def _():
+                v = both_terms(q, z)
+                for k in range(1, nz):
+                    straight(i, k).wait()
+                    v = v + rs[i, k].astype(F32)
+                v = v.astype(BF)
+                sum_gu[0, :, :, pl.ds(pl.multiple_of((q - nf) * COLS, COLS), COLS)] = v
+                squared(v)
+
+            return 0
+
         def each_gu(q, _):
             s = p - (ready(q) + 2)
 
             @pl.when(jnp.logical_and(s >= 0, s <= last))
             def _():
-                @pl.when(s == 0)
-                def _():
-                    over_gu(q).wait_recv()
-
                 event(Gu(q), s)
 
             return 0
 
         def each_d(k, _):
-            layer = 1 - k
             s = p - (first_down + 2 * k)
 
             @pl.when(jnp.logical_and(s >= 0, s <= last))
             def _():
-                @pl.when(s == 0)
-                def _():
-                    over_d(layer).wait_recv()
-
-                event(Down(layer), s)
+                event(Down(1 - k), s)
 
             return 0
 
-        lax.fori_loop(0, 2, each_d, 0)
-        lax.fori_loop(0, 2 * nf, each_gu, 0)
+        @pl.when(p >= ready(rings) + 2)
+        def _():
+            lax.fori_loop(0, DIRECT, each_direct, 0)
+
+        @pl.when(p >= first_down)
+        def _():
+            lax.fori_loop(0, 2, each_d, 0)
+
+        lax.fori_loop(0, rings, each_gu, 0)
 
     def grads(q):
         for b in range(nz):
             for c in range(2):
                 k = (b * 2 + c) * rows_g
-                tgu[q, 0, b, c] = acc_g[k : k + rows_g, :].astype(BF)
-                tgu[q, 1, b, c] = acc_u[k : k + rows_g, :].astype(BF)
+                for i in range(2):
+                    tgu[q, i, b, c] = acc_gu[k : k + rows_g, i * COLS : (i + 1) * COLS].astype(BF)
         over_gu(q).start()
 
     def wide_step(j, with_top):
@@ -431,11 +480,11 @@
             act = gate * sig
             by_up = (by_hid * act).astype(BF)
             by_gate = (by_hid * up * (sig + act * (1.0 - sig))).astype(BF)
-            acc_g[...] += dot_t(rows, by_gate)
-            acc_u[...] += dot_t(rows, by_up)
+            by_both = jnp.concatenate([by_gate, by_up], axis=1)
+            acc_gu[...] += dot_t(rows, by_both)
             if with_top:
                 acc_d[...] += dot_t(by_y, (act * up).astype(BF))
-                acc[at, :] += dot(by_gate, gt[0, cols, :]) + dot(by_up, gt[1, cols, :])
+                acc[at, :] += dot(by_both, gt[j])
             return 0
 
         return body
@@ -460,8 +509,7 @@
         return 0
 
     def zero():
-        acc_g[...] = jnp.zeros_like(acc_g)
-        acc_u[...] = jnp.zeros_like(acc_u)
+        acc_gu[...] = jnp.zeros_like(acc_gu)
 
     def phase(p, _):
         part_of = p % 2
@@ -492,6 +540,7 @@
                 over_d(1).start()
                 for c in later:
                     c.start()
+                early[4].wait()
                 lax.fori_loop(0, tiles, top_end, 0)
 
         @pl.when(jnp.logical_and(p >= first_down, p < first_low))
@@ -529,7 +578,7 @@
         events(p)
         return 0
 
-    lax.fori_loop(0, end_low + nz, phase, 0)
+    lax.fori_loop(0, end_low + WAIT + 1, phase, 0)
 
     all_ssq[me] = ssq[...]
 
@@ -545,31 +594,6 @@
 
     lax.fori_loop(1, n, tell, 0)
 
-    def left_gu(q, _):
-        over_gu(q).wait_send()
-
-        def one(s, _):
-            for way in range(2):
-                Gu(q).move(way, s).wait_send()
-            return 0
-
-        lax.fori_loop(0, last, one, 0)
-        return 0
-
-    def left_d(layer, _):
-        over_d(layer).wait_send()
-
-        def one(s, _):
-            for way in range(2):
-                Down(layer).move(way, s).wait_send()
-            return 0
-
-        lax.fori_loop(0, last, one, 0)
-        return 0
-
-    lax.fori_loop(0, 2 * nf, left_gu, 0)
-    lax.fori_loop(0, 2, left_d, 0)
-
     def told(k, _):
         scalar(k, (me + n - k) % n).wait()
         return 0
@@ -577,10 +601,10 @@
     lax.fori_loop(1, n, told, 0)
     total = jnp.sum(jnp.sum(jnp.sum(all_ssq[...], axis=0), axis=0, keepdims=True), axis=1, keepdims=True)
     count = 3 * 2 * dim * hidden
-    factor[...] = jnp.broadcast_to(jnp.minimum(1.0, 0.5 * lax.rsqrt(total / count + 1e-30)), factor.shape)
-
-
-def backward(n, h1, dy, a0, hid, gu, dt):
+    factor[0, 0] = jnp.max(jnp.minimum(1.0, 0.5 * lax.rsqrt(total / count + 1e-30)))
+
+
+def backward(n, h1, a1, dy, a0, hid, gu, dt):
     nz = n // 2
     tokens, dim = a0.shape
     hidden = dt.shape[2]
@@ -595,31 +619,31 @@
         out_shape=[
             jax.ShapeDtypeStruct((2, 2, rg, hidden), BF),
             jax.ShapeDtypeStruct((2, rd, dim), BF),
-            jax.ShapeDtypeStruct((8, 128), F32),
+            jax.ShapeDtypeStruct((1, 1), F32),
         ],
-        in_specs=[anyspace] * 6,
-        out_specs=[vmem] * 3,
+        in_specs=[anyspace] * 7,
+        out_specs=[vmem, vmem, pl.BlockSpec(memory_space=pltpu.SMEM)],
         scratch_shapes=[
             V(tokens, dim),
             V(tokens, dim),
             V(tokens, dim),
             W(tokens, dim),
             V(2, dim, hidden),
-            V(2, hidden, dim),
+            V(nf, 2 * COLS, dim),
             V(dim, hidden),
             V(3, TILE, hidden),
             V(2 * nf, 2, nz, 2, rg, COLS),
             V(2, nz, 2, rd, dim),
             V(2 * nf, 2, nz, rg, COLS),
             V(2, nz, rd, dim),
-            V(2 * nf, 2, last, 2, rg, COLS // 2),
+            V(2 * nf - DIRECT, 2, last, 2, rg, COLS // 2),
             V(2, 2, last, rd, dim // 2),
-            W(dim, COLS),
-            W(dim, COLS),
+            V(DIRECT, nz, 2, rg, COLS),
+            W(dim, 2 * COLS),
             W(dim, COLS),
             W(8, 128),
             W(n, 8, 128),
-            S(7),
+            S(8),
             S(3),
             S(2 * nf + 2),
             S(2 * nf + 2),
@@ -627,13 +651,15 @@
             S(2 * nf, 2, last),
             S(2, 2, last),
             S(2, 2, last),
+            S(DIRECT, nz),
+            S(DIRECT, nz),
             S(n),
             S(n),
         ],
         compiler_params=pltpu.CompilerParams(collective_id=1, has_side_effects=True, vmem_limit_bytes=VMEM_LIMIT),
         cost_estimate=pl.CostEstimate(flops=28 * tokens * dim * hidden, bytes_accessed=40 << 20, transcendentals=0),
         name="backward",
-    )(h1, dy, a0, hid, gu, dt)
+    )(h1, a1, dy, a0, hid, gu, dt)
 
 
 def adamw(w, m, v, g):
@@ -648,8 +674,8 @@
 
     def step(x, dy, *arrays):
         weights, m, v = (arrays[i : i + 3] for i in (0, 3, 6))
-        h1, hid, a0, gu, dt = forward(n, x[0], *weights)
-        sum_gu, sum_d, factor = backward(n, h1, dy[0], a0, hid, gu, dt)
+        h1, a1, hid, a0, gu, dt = forward(n, x[0], *weights)
+        sum_gu, sum_d, factor = backward(n, h1, a1, dy[0], a0, hid, gu, dt)
         gradients = [sum_gu[:, 0].astype(F32), sum_gu[:, 1].astype(F32), sum_d.astype(F32)]
         factor = factor[0, 0]
         new = [adamw(w.astype(F32), m, v, g * factor) for w, m, v, g in zip(weights, m, v, gradients, strict=True)]

time: 234 us -> 221 us (0.944)
  Pallas kernels: 226 us -> 214 us
    pallas_call x1, Pallas kernels: 160 us -> 151 us  [backward(): pl.pallas_call(functools.partial(backward_kernel, n), out_shape=[jax.Shap...]
    pallas_call x1, Pallas kernels: 66.4 us -> 62.9 us  [forward(): pl.pallas_call(functools.partial(forward_kernel, n), out_shape=[jax.Shape...]
where the time goes in v3:
time: 221 us; the launch traced here: 220 us
  Pallas kernels  214 us (97%)
  other arithmetic  6.08 us (3%)
    pallas_call x1, Pallas kernels, backward(): pl.pallas_call(functools.partial(backward_kernel, n), out_shape=[jax.Shap...  151 us
    pallas_call x1, Pallas kernels, forward(): pl.pallas_call(functools.partial(forward_kernel, n), out_shape=[jax.Shape...  62.9 us
    convert_element_type x2, other arithmetic, adamw(): return ((w - 0.02 * step).astype(BF), m, v)  6.08 us

profile of v3, /device:TPU:21, one launch (start us, length us, event | category | flops | bytes accessed | tf_op | source)
XLA Modules:
  0.0 220.5 jit_solution(4949407980808443102)
XLA Ops:
  0.6 62.9 %forward0.1 = (bf16[4096,512]{1,0:T(8,128)(2,1)}, bf16[4096,512]{1,0:T(8,128)(2,1)}, bf16[4096,1280]{1,0:T(8,128)(2,1)}, bf16[4096,512]{1,0:T(8,128)(2,1)}, bf16...) custom-call(bf16[4096,512]{1,0:T(8,128)(2,1)} %bitcast.25, bf16[2,32,1280]{2,1,0:T(8,128)(2,1)} %wg_ref.1, ...), custom_call_target="tpu_custom_call" | custom-call | flops 16106127360 | bytes 41943040 | tf_op jit(solution)/shard_map/forward0/pallas_call | solution.py:209
  63.5 0.0 copy-start
  63.6 0.0 copy-start.1
  63.6 150.8 %backward.1 = (bf16[2,2,32,1280]{3,2,1,0:T(8,128)(2,1)}, bf16[2,80,512]{2,1,0:T(8,128)(2,1)}, f32[1,1]{1,0:T(1,128)}) custom-call(bf16[4096,512]{1,0:T(8,128)(2,1)} %get-tuple-element.18.h1_hbm, bf16[4096,512]{1,0:T(8,128)(2,1)} %get-tuple-element.19.a1_hbm, bf16[4096,512]{1,0:T(8,128)(2,1)} %bitcast.26, bf16[4096,512]{1,0:T(8,128)(2,1)} %get-tuple-element.20.a0_hbm, ...), custom_call_target="tpu_custom_call" | custom-call | flops 75161927680 | bytes 41943040 | tf_op jit(solution)/shard_map/backward/pallas_call | solution.py:617
  214.4 0.0 copy-done
  214.4 0.0 copy-done.1
  214.4 2.6 %fusion.8 = (bf16[2,80,512]{2,1,0:T(8,128)(2,1)}, f32[2,80,512]{2,1,0:T(8,128)}, f32[2,80,512]{2,1,0:T(8,128)}) fusion(bf16[2,80,512]{2,1,0:T(8,128)(2,1)S(1)} %copy-done.1, f32[]{:T(128)} %bitcast.2, bf16[2,80,512]{2,1,0:T(8,128)(2,1)} %get-tuple-element.26, f32[2,80,512]{2,1,0:T(8,128)S(1)} %copy-done, f32[2,80,512]{2,1,0:T(8,128)} %param.18), kind=kLoop, calls=%fused_computation.17 | loop fusion | flops 1392640 | bytes 1802244 | tf_op jit(solution)/shard_map/convert_element_type | solution.py:669
  217.0 3.4 %fusion.2 = (bf16[2,32,1280]{2,1,0:T(8,128)(2,1)}, f32[2,32,1280]{2,1,0:T(8,128)}, f32[2,32,1280]{2,1,0:T(8,128)}, bf16[2,32,1280]{2,1,0:T(8,128)(2,1)}, f32[2,32,1280]{2,1,0:T(8,128)}, /*index=5*/f32[2,32,1280]{2,1,0:T(8,128)}) fusion(bf16[2,32,1280]{2,1,0:T(8,128)(2,1)} %wg_ref.1, f32[]{:T(128)} %bitcast.2, f32[2,32,1280]{2,1,0:T(8,128)} %param.19, ...), kind=kLoop, calls=%fused_computation.11 | loop fusion | flops 2785280 | bytes 3604484 | tf_op jit(solution)/shard_map/convert_element_type | solution.py:669
Async XLA Ops:
  63.5 150.8 %copy-start = (f32[2,80,512]{2,1,0:T(8,128)S(1)}, f32[2,80,512]{2,1,0:T(8,128)}, u32[]{:S(2)}) copy-start(f32[2,80,512]{2,1,0:T(8,128)} %param.21) | copy-start | bytes 983044
  63.6 150.8 %copy-start.1 = (bf16[2,80,512]{2,1,0:T(8,128)(2,1)S(1)}, bf16[2,80,512]{2,1,0:T(8,128)(2,1)}, u32[]{:S(2)}) copy-start(bf16[2,80,512]{2,1,0:T(8,128)(2,1)} %wd_ref.1) | copy-start | bytes 491524
